TPU v7x, 128 devices: a whole 4x4x4 slice. The times are simulated.
128 devices in a mesh: dp: 1, tp: 2 (over core), sp: 64 (over z, y, x).
Axes of the slice: x: 4, y: 4, z: 4, core: 2. Of those that a mesh axis runs over, the one named last changes fastest.
Arguments:
- hidden: bfloat16 [4, 8192], P('dp')
- norm_gain: float32 [8192], replicated
- w_query: bfloat16 [8192, 8192], P(None, 'tp')
- w_key: bfloat16 [8192, 1024], P(None, 'tp')
- w_value: bfloat16 [8192, 1024], P(None, 'tp')
- w_out: bfloat16 [8192, 8192], P('tp')
- k_cache: bfloat16 [4, 32768, 8, 128], P('dp', 'sp', 'tp')
- v_cache: bfloat16 [4, 32768, 8, 128], P('dp', 'sp', 'tp')
- positions: int32 [4], P('dp')
Outputs:
- output 1: bfloat16 [4, 8192], P('dp')
- output 2: bfloat16 [4, 32768, 8, 128], P('dp', 'sp', 'tp')
- output 3: bfloat16 [4, 32768, 8, 128], P('dp', 'sp', 'tp')
All inputs are finite; a program needn't handle non-finite values.
Results may differ from a plain program's by a relative error of at most 0.00424275.
Values sent between devices are 32-bit elements.
A program may use at most 1 GiB of HBM per device.

v0:
```python
import jax
import jax.numpy as jnp
from jax import lax
from jax.sharding import PartitionSpec as P

ROPE_BASE = 1000000.0
EPS = 1e-5
NEG_BIG = -1e30


def rotary(tensor, positions):
    half_dim = tensor.shape[-1] // 2
    inv_freq = 1.0 / (ROPE_BASE ** (jnp.arange(half_dim, dtype=jnp.float32) * 2.0 / tensor.shape[-1]))
    angles = positions.astype(jnp.float32)[:, None, None] * inv_freq[None, None, :]
    cosine = jnp.cos(angles)
    sine_val = jnp.sin(angles)
    first_half = tensor[..., :half_dim]
    second_half = tensor[..., half_dim:]
    return jnp.concatenate([first_half * cosine - second_half * sine_val, first_half * sine_val + second_half * cosine], axis=-1)


def solution(mesh):
    def local_step(hidden, norm_gain, w_query, w_key, w_value, w_out, k_cache, v_cache, positions):
        batch_size, seq_local, kv_local, head_dim = k_cache.shape
        q_local = w_query.shape[1] // head_dim
        group_size = q_local // kv_local
        resid_f32 = hidden.astype(jnp.float32)
        normed = (resid_f32 * lax.rsqrt(jnp.mean(resid_f32 * resid_f32, axis=-1, keepdims=True) + EPS) * norm_gain).astype(jnp.bfloat16)
        q_proj = jnp.dot(normed, w_query, preferred_element_type=jnp.float32).reshape(batch_size, q_local, head_dim)
        k_proj = jnp.dot(normed, w_key, preferred_element_type=jnp.float32).reshape(batch_size, kv_local, head_dim)
        v_new = jnp.dot(normed, w_value, preferred_element_type=jnp.float32).astype(jnp.bfloat16).reshape(batch_size, kv_local, head_dim)
        q_rot = rotary(q_proj, positions).astype(jnp.bfloat16).reshape(batch_size, kv_local, group_size, head_dim)
        k_new = rotary(k_proj, positions).astype(jnp.bfloat16)
        slot_pos = lax.axis_index("sp") * seq_local + jnp.arange(seq_local)
        slot_mask = (slot_pos[None, :] == positions[:, None])[:, :, None, None]
        k_updated = jnp.where(slot_mask, k_new[:, None], k_cache)
        v_updated = jnp.where(slot_mask, v_new[:, None], v_cache)
        scores = jnp.einsum("bkgd,bskd->bkgs", q_rot, k_updated, preferred_element_type=jnp.float32) * (head_dim ** -0.5)
        valid_mask = (slot_pos[None, :] <= positions[:, None])[:, None, None, :]
        scores = jnp.where(valid_mask, scores, NEG_BIG)
        local_max = jnp.max(scores, axis=-1, keepdims=True)
        exp_weights = jnp.where(valid_mask, jnp.exp(scores - local_max), 0.0)
        local_sum = jnp.sum(exp_weights, axis=-1, keepdims=True)
        local_acc = jnp.einsum("bkgs,bskd->bkgd", exp_weights.astype(jnp.bfloat16), v_updated, preferred_element_type=jnp.float32)
        block_stats = jnp.concatenate([local_acc, local_sum, local_max], axis=-1)
        gathered = lax.all_gather(block_stats, "sp")
        all_max = gathered[..., head_dim + 1:]
        global_max = jnp.max(all_max, axis=0)
        rescale = jnp.exp(all_max - global_max)
        total_sum = jnp.sum(gathered[..., head_dim:head_dim + 1] * rescale, axis=0)
        total_acc = jnp.sum(gathered[..., :head_dim] * rescale, axis=0)
        attn_out = (total_acc / total_sum).astype(jnp.bfloat16).reshape(batch_size, q_local * head_dim)
        part_proj = jnp.dot(attn_out, w_out, preferred_element_type=jnp.float32)
        proj_out = lax.psum(part_proj, "tp")
        return (resid_f32 + proj_out).astype(jnp.bfloat16), k_updated, v_updated

    cache_spec = P("dp", "sp", "tp", None)
    specs_in = (P("dp", None), P(None), P(None, "tp"), P(None, "tp"), P(None, "tp"), P("tp", None), cache_spec, cache_spec, P("dp"))
    specs_out = (P("dp", None), cache_spec, cache_spec)
    return jax.shard_map(local_step, mesh=mesh, in_specs=specs_in, out_specs=specs_out, check_vma=False)
```

profile of v0, /device:TPU:1, one launch (start us, length us, event | category | flops | bytes accessed | tf_op | source)
XLA Modules:
  0.0 209.1 jit_solution(4956887225040707592)
XLA Ops:
  7.2 0.7 convert_element_type.35
  7.9 1.0 fusion.14
  8.9 0.7 broadcast_compare_fusion.1
  9.7 4.7 %convolution_convert_fusion = bf16[4,512]{1,0:T(4,128)(2,1)S(1)} fusion(bf16[8192,512]{1,0:T(8,128)(2,1)} %param.13, bf16[4,8192]{1,0:T(4,128)(2,1)} %param.9, f32[8192]{0:T(1024)} %param.10, f32[4]{0:T(128)S(1)} %add_rsqrt_fusion), kind=kOutput, calls=%fused_computation.15 | convolution fusion | flops 33687552 | bytes 8491024 | tf_op jit(solution)/shard_map/dot_general | solution.py:31
  14.4 4.6 %fusion.34 = f32[4,512]{1,0:T(4,128)S(1)} fusion(bf16[8192,512]{1,0:T(8,128)(2,1)} %param.12, bf16[4,8192]{1,0:T(4,128)(2,1)S(1)} %copy-done.2, f32[8192]{0:T(1024)S(1)} %copy-done.3, f32[4]{0:T(128)S(1)} %add_rsqrt_fusion), kind=kOutput, calls=%fused_computation.55 | convolution fusion | flops 33685504 | bytes 8495120 | tf_op jit(solution)/shard_map/dot_general | solution.py:30
  19.0 22.7 %convolution_bitcast_fusion = f32[1,4,32,128]{3,1,2,0:T(4,128)S(1)} fusion(bf16[8192,4096]{1,0:T(8,128)(2,1)} %param.11, bf16[4,8192]{1,0:T(4,128)(2,1)S(1)} %copy-done.2, f32[8192]{0:T(1024)S(1)} %copy-done.3, f32[4]{0:T(128)S(1)} %add_rsqrt_fusion), kind=kOutput, calls=%fused_computation.14 | convolution fusion | flops 268566528 | bytes 67272720 | tf_op jit(solution)/shard_map/dot_general | solution.py:29
  42.1 9.4 %broadcast_select_fusion = (bf16[4,512,4,128]{3,2,1,0:T(4,128)(2,1)S(1)}, bf16[4,512,4,128]{3,2,1,0:T(4,128)(2,1)S(1)}) fusion(bf16[4,512,4,128]{3,2,1,0:T(4,128)(2,1)} %param.16, pred[4,512]{1,0:T(4,128)(4,1)S(1)} %get-tuple-element.10, bf16[4,4,128]{2,1,0:T(4,128)(2,1)S(1)} %broadcast_in_dim.69, bf16[4,512,4,128]{3,2,1,0:T(4,128)(2,1)} %param.15, ...), kind=kLoop, calls=%fused_computation.10 | loop fusion | flops 2097152 | bytes 8398848 | tf_op jit(solution)/shard_map/jit(_where)/select_n | solution.py:37
  51.5 1.3 copy-done.1
  52.8 0.8 fusion.37
  53.6 0.2 fusion.12
  53.8 0.5 fusion.2
  54.3 0.2 copy.29
  54.4 0.2 copy.30
  54.6 0.8 pad_maximum_fusion
  55.4 0.2 all-reduce.2.cloned.1.call-start
  55.6 80.9 %all-gather.3.cloned.1.call-done = f32[256,4,8,130]{3,2,1,0:T(8,128)} async-done(((f32[4,4,8,130]{3,2,1,0:T(8,128)}), f32[256,4,8,130]{3,2,1,0:T(8,128)}) %all-gather.3.cloned.1.call-update) | async-done | bytes 4259856 | tf_op jit(solution)/shard_map/all_gather | solution.py:46
  136.5 3.4 %slice_reduce_fusion = f32[4,4,8]{2,1,0:T(4,128)S(1)} fusion(f32[64,4,4,8,130]{4,3,2,1,0:T(8,128)} %bitcast.23), kind=kLoop, calls=%fused_computation.5 | loop fusion | flops 8064 | bytes 33280 | tf_op jit(solution)/shard_map/reduce_max | solution.py:48
  140.0 6.6 %fusion = (f32[4,4,8]{2,1,0:T(4,128)S(1)}, f32[64,4,4,8,1]{4,3,2,1,0:T(8,128)}) fusion(f32[64,4,4,8,130]{4,3,2,1,0:T(8,128)} %bitcast.24, f32[4,4,8]{2,1,0:T(4,128)S(1)} %slice_reduce_fusion), kind=kLoop, calls=%fused_computation.1 | loop fusion | flops 24448 | bytes 99328 | tf_op jit(solution)/shard_map/reduce_sum | solution.py:50
  146.6 3.7 %copy.31 = f32[64,4,4,8,1]{0,3,4,2,1:T(8,128)S(1)} copy(f32[64,4,4,8,1]{4,3,2,1,0:T(8,128)} %get-tuple-element.4) | data formatting | bytes 65536 | tf_op jit(solution)/shard_map/exp | solution.py:49
  150.3 0.3 copy.32
  150.6 2.9 %fusion.1 = f32[4,4,8,128]{3,2,1,0:T(8,128)S(1)} fusion(f32[64,4,4,8,130]{4,3,2,1,0:T(8,128)} %bitcast.25, f32[64,4,4,8]{3,2,1,0:T(4,128)S(1)} %copy.32), kind=kLoop, calls=%fused_computation.3 | loop fusion | flops 2080768 | bytes 4292608 | tf_op jit(solution)/shard_map/reduce_sum | solution.py:51
  153.6 23.3 %fusion.24 = f32[4,8192]{1,0:T(4,128)} fusion(bf16[4096,8192]{1,0:T(8,128)(2,1)} %param.14, bf16[1,4,32,128]{3,2,1,0:T(8,128)(2,1)S(1)} %fusion.30), kind=kOutput, calls=%fused_computation.36 | convolution fusion | flops 268435456 | bytes 67272704 | tf_op jit(solution)/shard_map/dot_general | solution.py:53
  176.9 23.7 %all-reduce.2.cloned.1.call-done = f32[4,8192]{1,0:T(4,128)} async-done(((f32[4,8192]{1,0:T(4,128)}), f32[4,8192]{1,0:T(4,128)}) %all-reduce.2.cloned.1.call-update) | async-done | bytes 131088 | tf_op jit(solution)/shard_map/psum | solution.py:54
  200.7 1.6 fusion.17
  (21 shorter events, 0.6 us)
Async XLA Ops:
  7.2 129.4 %all-gather.3.cloned.1.call-start = ((), (), s32[]{:S(2)}) async-start(), calls=%async_computation.1 | async-start | bytes 8519680 | tf_op jit(solution)/shard_map/all_gather | solution.py:46
  9.7 4.7 %copy-start.2 = (bf16[4,8192]{1,0:T(4,128)(2,1)S(1)}, bf16[4,8192]{1,0:T(4,128)(2,1)}, u32[]{:S(2)}) copy-start(bf16[4,8192]{1,0:T(4,128)(2,1)} %param.9) | copy-start | bytes 196612
  9.7 4.7 %copy-start.3 = (f32[8192]{0:T(1024)S(1)}, f32[8192]{0:T(1024)}, u32[]{:S(2)}) copy-start(f32[8192]{0:T(1024)} %param.10) | copy-start | bytes 98308
  51.5 1.3 copy-start.1
  51.5 88.5 %copy-start = (bf16[4,512,4,128]{3,2,1,0:T(4,128)(2,1)}, bf16[4,512,4,128]{3,2,1,0:T(4,128)(2,1)S(1)}, u32[]{:S(2)}) copy-start(bf16[4,512,4,128]{3,2,1,0:T(4,128)(2,1)S(1)} %get-tuple-element.11) | copy-start | bytes 6291460
  55.4 145.3 %all-reduce.2.cloned.1.call-start = ((), (), s32[]{:S(2)}) async-start(), calls=%async_computation | async-start | bytes 262144 | tf_op jit(solution)/shard_map/psum | solution.py:54
Sparse Core Ops, SparseCore 0:
  55.5 80.9 all-gather.2
  177.1 23.5 all-reduce.1
where the time goes:
time: 210 us; the launch traced here: 209 us
  waiting for transfers between devices  105 us (50%)
  matrix products  56.5 us (27%)
  other arithmetic  27.8 us (13%)
  between operations  14.1 us (7%)
  local copies, waits for them, and re-layouts  5.69 us (3%)
    all_gather x1, waiting for transfers between devices, local_step(): gathered = lax.all_gather(block_stats, 'sp')  80.9 us
    psum x1, waiting for transfers between devices, local_step(): proj_out = lax.psum(part_proj, 'tp')  23.7 us
    dot_general x1, matrix products, local_step(): part_proj = jnp.dot(attn_out, w_out, preferred_element_type=jnp.float32)  23.3 us
    dot_general x1, matrix products, local_step(): jnp.dot(normed, w_query, preferred_element_type=jnp.float32)  22.7 us
    select_n x1, other arithmetic, local_step(): v_updated = jnp.where(slot_mask, v_new[:, None], v_cache)  9.43 us
    reduce_sum x1, other arithmetic, local_step(): total_sum = jnp.sum(gathered[..., head_dim:head_dim + 1] * rescale, axis=0)  6.65 us
    dot_general x1, matrix products, local_step(): jnp.dot(normed, w_value, preferred_element_type=jnp.float32)  4.7 us
    dot_general x1, matrix products, local_step(): jnp.dot(normed, w_key, preferred_element_type=jnp.float32)  4.61 us
  transfers between devices with their start and end apart: 2, of which 2 were waited for; matrix products, arithmetic and copies ran while one was open for 0% of the time, Pallas kernels for 0%

commit v1 on v0

v1 whole, which is shorter than its diff:
```python
import functools

import jax
import jax.numpy as jnp
import numpy as np
from jax import lax
from jax.experimental import pallas as pl
from jax.experimental.pallas import tpu as pltpu
from jax.sharding import PartitionSpec as P

ROPE_BASE = 1000000.0
EPS = 1e-5
NEG_BIG = -3.0e38
SIDE = 4
PLANE = SIDE * SIDE
AXES = ("x", "y", "z")
DIMS = (48, 40, 40)
STARTS = (0, 48, 88)
CHUNKS = 8
BF16 = jnp.bfloat16
F32 = jnp.float32


def sum_bytes(ref, sem):
    pltpu.make_async_copy(ref, ref, sem).wait()


def attention_kernel(
    hidden_hbm, gain_hbm, freq_hbm, pos_hbm, wq_hbm, wk_hbm, wv_hbm, wo_hbm, k_hbm, v_hbm,
    out_ref, knew_ref, vnew_ref,
    hid, gain, freq, wq, wk, wv, wo, kbuf, vbuf, gathered, fresh, rows, x0, x1, x2, orow, ypart, ypeer, yall,
    pos, sems, wq_sems, part_send, part_recv, qsend, qrecv, tpsend, tprecv, ysend, yrecv,
):
    batch, d_model = hid.shape
    head = 128
    seq_local = kbuf.shape[1] // 4
    me = lax.axis_index("sp")
    core = lax.axis_index("tp")
    lx = lax.rem(me, SIDE)
    ly = lax.rem(me // SIDE, SIDE)
    lz = me // PLANE
    cell = lax.rem(me, PLANE)
    line = {"x": lx, "y": ly, "z": lz}
    stride = {"x": 1, "y": SIDE, "z": PLANE}

    def line_peer(axis, step):
        here = line[axis]
        return me + (lax.rem(here + step, SIDE) - here) * stride[axis]

    def plane_peer(step_y, step_x):
        return lz * PLANE + lax.rem(ly + step_y, SIDE) * SIDE + lax.rem(lx + step_x, SIDE)

    plane_steps = sorted(
        [(a, b) for a in range(SIDE) for b in range(SIDE) if (a, b) != (0, 0)],
        key=lambda s: -(min(s[0], SIDE - s[0]) + min(s[1], SIDE - s[1])),
    )

    barrier = pltpu.get_barrier_semaphore()
    for a, b in plane_steps:
        pl.semaphore_signal(barrier, inc=1, device_id={"sp": plane_peer(a, b), "tp": core})
    for step in (2, 1, 3):
        pl.semaphore_signal(barrier, inc=1, device_id={"sp": line_peer("z", step), "tp": core})
    pl.semaphore_signal(barrier, inc=1, device_id={"sp": me, "tp": 1 - core})

    cp_hid = pltpu.make_async_copy(hidden_hbm, hid, sems.at[0])
    cp_gain = pltpu.make_async_copy(gain_hbm, gain, sems.at[1])
    cp_pos = pltpu.make_async_copy(pos_hbm, pos, sems.at[2])
    cp_freq = pltpu.make_async_copy(freq_hbm, freq, sems.at[3])
    for cp in (cp_hid, cp_gain, cp_pos, cp_freq):
        cp.start()
    q_cols = pl.ds(pl.multiple_of(cell * 256, 256), 256)
    q_rows = d_model // CHUNKS
    cp_wq = [
        pltpu.make_async_copy(
            wq_hbm.at[pl.ds(c * q_rows, q_rows), q_cols], wq.at[pl.ds(c * q_rows, q_rows), :], wq_sems.at[c]
        )
        for c in range(CHUNKS)
    ]
    kv_depth = d_model // SIDE
    kv_rows = pl.ds(pl.multiple_of(lx * kv_depth, kv_depth), kv_depth)
    kv_cols = pl.ds(pl.multiple_of(ly * head, head), head)
    cp_wk = pltpu.make_async_copy(wk_hbm.at[kv_rows, kv_cols], wk, sems.at[4])
    cp_wv = pltpu.make_async_copy(wv_hbm.at[kv_rows, kv_cols], wv, sems.at[5])
    for cp in cp_wq:
        cp.start()
    cp_wk.start()
    cp_wv.start()
    cp_k = pltpu.make_async_copy(k_hbm, kbuf, sems.at[6])
    cp_v = pltpu.make_async_copy(v_hbm, vbuf, sems.at[7])
    n_cols = wo.shape[1]
    o_cols = pl.ds(pl.multiple_of(cell * n_cols, n_cols), n_cols)
    cp_wo = pltpu.make_async_copy(wo_hbm.at[:, o_cols], wo, sems.at[8])

    cp_hid.wait()
    cp_gain.wait()
    resid = hid[...].astype(F32)
    scale = lax.rsqrt(jnp.mean(resid * resid, axis=-1, keepdims=True) + EPS)
    normed = (resid * scale * gain[...]).astype(BF16)

    cp_pos.wait()
    cp_freq.wait()
    row4 = lax.broadcasted_iota(jnp.int32, (batch, head), 0)
    lane4 = lax.broadcasted_iota(jnp.int32, (batch, head), 1)
    pos_rows = jnp.zeros((batch, head), jnp.int32)
    for b in range(batch):
        pos_rows = jnp.where(row4 == b, pos[b], pos_rows)
    angles = pos_rows.astype(F32) * freq[...]
    cosine = jnp.cos(angles)
    sine = jnp.sin(angles)
    sine = jnp.where(lane4 < head // 2, -sine, sine)

    def rotate(u):
        return u * cosine + pltpu.roll(u, head // 2, axis=1) * sine

    q_acc = jnp.zeros((batch, 256), F32)
    for c in range(CHUNKS):
        cp_wq[c].wait()
        q_acc += jnp.dot(
            normed[:, c * q_rows:(c + 1) * q_rows], wq[c * q_rows:(c + 1) * q_rows, :], preferred_element_type=F32
        )
    cp_k.start()
    cp_v.start()
    rows[...] = normed.astype(F32)
    normed_kv = rows[:, kv_rows].astype(BF16)
    cp_wk.wait()
    k_part = jnp.dot(normed_kv, wk[...], preferred_element_type=F32)
    cp_wv.wait()
    v_part = jnp.dot(normed_kv, wv[...], preferred_element_type=F32)
    q_lo = rotate(q_acc[:, :head]).astype(BF16).astype(F32)
    q_hi = rotate(q_acc[:, head:]).astype(BF16).astype(F32)
    mine = pl.ds(pl.multiple_of(cell * 16, 16), 16)
    gathered[mine, :] = jnp.concatenate([q_lo, q_hi, k_part, v_part], axis=0)

    pl.semaphore_wait(barrier, PLANE - 1 + SIDE - 1 + 1)
    for a, b in plane_steps:
        pltpu.make_async_remote_copy(
            src_ref=gathered.at[mine], dst_ref=gathered.at[mine], send_sem=qsend, recv_sem=qrecv,
            device_id={"sp": plane_peer(a, b), "tp": core},
        ).start()
    cp_wo.start()
    sum_bytes(gathered.at[pl.ds(0, 16 * (PLANE - 1))], qrecv)

    cos_all = jnp.concatenate([cosine] * 4, axis=0)
    sin_all = jnp.concatenate([sine] * 4, axis=0)
    k_sum, v_sum = [], []
    for j in range(4):
        k_sum.append(sum(gathered[(4 * j + i) * 16 + 8:(4 * j + i) * 16 + 12, :] for i in range(4)))
        v_sum.append(sum(gathered[(4 * j + i) * 16 + 12:(4 * j + i) * 16 + 16, :] for i in range(4)))
    k_all = jnp.concatenate(k_sum, axis=0)
    v_all = jnp.concatenate(v_sum, axis=0)
    k_all = k_all * cos_all + pltpu.roll(k_all, head // 2, axis=1) * sin_all
    fresh[0:16, :] = k_all.astype(BF16).astype(F32)
    fresh[16:32, :] = v_all.astype(BF16).astype(F32)

    cols = seq_local * 4
    row_head = lax.rem(lax.broadcasted_iota(jnp.int32, (32, cols), 0), 16) // 4
    col_id = lax.broadcasted_iota(jnp.int32, (32, cols), 1)
    same_head = row_head == lax.rem(col_id, 4)
    new_row = lax.rem(lax.broadcasted_iota(jnp.int32, (32, 16), 0), 16) // 4
    new_head = new_row == lax.broadcasted_iota(jnp.int32, (32, 16), 1)
    ones16 = lax.broadcasted_iota(jnp.int32, (32, 16), 1) * 0
    base = me * seq_local
    pad = jnp.zeros((12, head), F32)
    dims_last = (((1,), (1,)), ((), ()))
    cp_k.wait()
    cp_v.wait()
    acc_rows, m_rows, l_rows = [], [], []
    for b in range(batch):
        k_b = jnp.concatenate([fresh[pl.ds(b, 4, stride=4), :], pad], axis=0).astype(BF16)
        v_b = jnp.concatenate([fresh[pl.ds(16 + b, 4, stride=4), :], pad], axis=0).astype(BF16)
        knew_ref[b] = k_b[0:4]
        vnew_ref[b] = v_b[0:4]
        q_b = jnp.concatenate(
            [gathered[pl.ds(b, 16, stride=16), :], gathered[pl.ds(4 + b, 16, stride=16), :]], axis=0
        ).astype(BF16)
        limit = (pos[b] - base) * 4
        valid = jnp.logical_and(same_head, col_id < limit)
        valid_new = jnp.logical_and(
            new_head, jnp.logical_and(ones16 + limit >= 0, ones16 + limit < cols)
        )
        s = lax.dot_general(q_b, kbuf[b], dims_last, preferred_element_type=F32) * (head ** -0.5)
        s_new = lax.dot_general(q_b, k_b, dims_last, preferred_element_type=F32) * (head ** -0.5)
        s = jnp.where(valid, s, NEG_BIG)
        s_new = jnp.where(valid_new, s_new, NEG_BIG)
        m = jnp.maximum(jnp.max(s, axis=-1, keepdims=True), jnp.max(s_new, axis=-1, keepdims=True))
        p = jnp.where(valid, jnp.exp(s - m), 0.0)
        p_new = jnp.where(valid_new, jnp.exp(s_new - m), 0.0)
        l_rows.append(jnp.sum(p, axis=-1, keepdims=True) + jnp.sum(p_new, axis=-1, keepdims=True))
        m_rows.append(m)
        acc_rows.append(
            jnp.dot(p.astype(BF16), vbuf[b], preferred_element_type=F32)
            + jnp.dot(p_new.astype(BF16), v_b, preferred_element_type=F32)
        )
    acc_t = jnp.concatenate(acc_rows, axis=0).T
    m_col = jnp.concatenate(m_rows, axis=0)
    l_col = jnp.concatenate(l_rows, axis=0)
    lane = lax.broadcasted_iota(jnp.int32, (128, 128), 1)
    stat_t = jnp.where(lane == 0, m_col, l_col).T[0:8]

    parts = (x0, x1, x2)

    def send_part(p, t):
        axis = AXES[(p + t) % 3]
        slot = parts[p].at[t, line[axis]]
        for step in (2, 1, 3):
            pltpu.make_async_remote_copy(
                src_ref=slot, dst_ref=slot, send_sem=part_send.at[p, t], recv_sem=part_recv.at[p, t],
                device_id={"sp": line_peer(axis, step), "tp": core},
            ).start()

    for p in range(3):
        axis = AXES[p]
        parts[p][0, line[axis], 0:DIMS[p], :] = acc_t[STARTS[p]:STARTS[p] + DIMS[p]]
        parts[p][0, line[axis], DIMS[p]:DIMS[p] + 8, :] = stat_t
    for p in range(3):
        send_part(p, 0)
    o_parts = []
    for t in range(3):
        for p in range(3):
            ref = parts[p]
            sum_bytes(ref.at[t, pl.ds(0, SIDE - 1)], part_recv.at[p, t])
            stats = [ref[t, i, DIMS[p]:DIMS[p] + 8, :] for i in range(SIDE)]
            ms = [st[0:1] for st in stats]
            top = jnp.maximum(jnp.maximum(ms[0], ms[1]), jnp.maximum(ms[2], ms[3]))
            fac = [jnp.exp(mi - top) for mi in ms]
            acc = sum(ref[t, i, 0:DIMS[p], :] * fac[i] for i in range(SIDE))
            total = sum(stats[i][1:2] * fac[i] for i in range(SIDE))
            if t < 2:
                slot = line[AXES[(p + t + 1) % 3]]
                ref[t + 1, slot, 0:DIMS[p], :] = acc
                row8 = lax.broadcasted_iota(jnp.int32, (8, 128), 0)
                ref[t + 1, slot, DIMS[p]:DIMS[p] + 8, :] = jnp.where(row8 == 0, top, total)
                send_part(p, t + 1)
            else:
                o_parts.append(acc / total)
    orow[...] = jnp.concatenate(o_parts, axis=0).T

    attn = jnp.concatenate(
        [orow[pl.ds(h // 2 + 16 * (h % 2), batch, stride=32), :] for h in range(32)], axis=1
    ).astype(BF16)
    cp_wo.wait()
    o_rows = wo.shape[0] // CHUNKS
    y = jnp.zeros((batch, n_cols), F32)
    for c in range(CHUNKS):
        y += jnp.dot(
            attn[:, c * o_rows:(c + 1) * o_rows], wo[c * o_rows:(c + 1) * o_rows, :], preferred_element_type=F32
        )
    ypart[...] = y
    cp_tp = pltpu.make_async_remote_copy(
        src_ref=ypart, dst_ref=ypeer, send_sem=tpsend, recv_sem=tprecv, device_id={"sp": me, "tp": 1 - core}
    )
    cp_tp.start()
    cp_tp.wait_recv()
    yall[cell] = ypart[...] + ypeer[...]
    for a, b in plane_steps:
        pltpu.make_async_remote_copy(
            src_ref=yall.at[cell], dst_ref=yall.at[cell], send_sem=ysend, recv_sem=yrecv,
            device_id={"sp": plane_peer(a, b), "tp": core},
        ).start()
    sum_bytes(yall.at[pl.ds(0, PLANE - 1)], yrecv)
    for i in range(PLANE):
        out_ref[:, i * n_cols:(i + 1) * n_cols] = (
            hid[:, i * n_cols:(i + 1) * n_cols].astype(F32) + yall[i]
        ).astype(BF16)

    cp_tp.wait_send()
    sum_bytes(gathered.at[pl.ds(0, 16 * (PLANE - 1))], qsend)
    sum_bytes(yall.at[pl.ds(0, PLANE - 1)], ysend)
    for t in range(3):
        for p in range(3):
            sum_bytes(parts[p].at[t, pl.ds(0, SIDE - 1)], part_send.at[p, t])


def update_kernel(base_unused, y_ref, k_ref, v_ref, knew_ref, vnew_ref, pos_ref, out_ref, ko_ref, vo_ref, sems, row_sems):
    batch, seq_local = k_ref.shape[0], k_ref.shape[1]
    base = lax.axis_index("sp") * seq_local
    bulk = []
    for b in range(batch):
        bulk.append(pltpu.make_async_copy(k_ref.at[b], ko_ref.at[b], sems.at[0, b]))
        bulk.append(pltpu.make_async_copy(v_ref.at[b], vo_ref.at[b], sems.at[1, b]))
    for cp in bulk:
        cp.start()
    out_ref[...] = y_ref[...]
    for b in range(batch):
        bulk[2 * b].wait()
        bulk[2 * b + 1].wait()
        spot = pos_ref[b] - base

        @pl.when(jnp.logical_and(spot >= 0, spot < seq_local))
        def _():
            cp_k = pltpu.make_async_copy(knew_ref.at[b], ko_ref.at[b, spot], row_sems.at[0])
            cp_v = pltpu.make_async_copy(vnew_ref.at[b], vo_ref.at[b, spot], row_sems.at[1])
            cp_k.start()
            cp_v.start()
            cp_k.wait()
            cp_v.wait()


def solution(mesh):
    def local_step(hidden, norm_gain, w_query, w_key, w_value, w_out, k_cache, v_cache, positions):
        batch, seq_local, kv_local, head = k_cache.shape
        d_model = hidden.shape[1]
        n_cols = w_out.shape[1] // PLANE
        half = np.arange(head // 2, dtype=np.float32) * np.float32(2.0) / np.float32(head)
        inv = (np.float32(1.0) / np.power(np.float32(ROPE_BASE), half)).astype(np.float32)
        freq = jnp.asarray(np.concatenate([inv, inv])[None, :])
        flat = (batch, seq_local * kv_local, head)
        hbm = pl.BlockSpec(memory_space=pltpu.HBM)
        vmem = pl.BlockSpec(memory_space=pltpu.VMEM)
        dma = pltpu.SemaphoreType.DMA
        y, k_new, v_new = pl.pallas_call(
            attention_kernel,
            out_shape=[
                jax.ShapeDtypeStruct(hidden.shape, BF16),
                jax.ShapeDtypeStruct((batch, kv_local, head), BF16),
                jax.ShapeDtypeStruct((batch, kv_local, head), BF16),
            ],
            in_specs=[hbm] * 10,
            out_specs=[vmem] * 3,
            scratch_shapes=[
                pltpu.VMEM(hidden.shape, BF16),
                pltpu.VMEM((1, d_model), F32),
                pltpu.VMEM((1, head), F32),
                pltpu.VMEM((d_model, 256), BF16),
                pltpu.VMEM((d_model // SIDE, head), BF16),
                pltpu.VMEM((d_model // SIDE, head), BF16),
                pltpu.VMEM((w_out.shape[0], n_cols), BF16),
                pltpu.VMEM(flat, BF16),
                pltpu.VMEM(flat, BF16),
                pltpu.VMEM((PLANE * 16, head), F32),
                pltpu.VMEM((32, head), F32),
                pltpu.VMEM((batch, d_model), F32),
                *[pltpu.VMEM((3, SIDE, d + 8, 128), F32) for d in DIMS],
                pltpu.VMEM((128, 128), F32),
                pltpu.VMEM((batch, n_cols), F32),
                pltpu.VMEM((batch, n_cols), F32),
                pltpu.VMEM((PLANE, batch, n_cols), F32),
                pltpu.SMEM((batch,), jnp.int32),
                dma((9,)),
                dma((CHUNKS,)),
                dma((3, 3)),
                dma((3, 3)),
                dma, dma, dma, dma, dma, dma,
            ],
            compiler_params=pltpu.CompilerParams(
                collective_id=0, has_side_effects=True, vmem_limit_bytes=30 << 20
            ),
            cost_estimate=pl.CostEstimate(flops=20_000_000_000, bytes_accessed=20_000_000, transcendentals=0),
            name="attention_step",
        )(
            hidden, norm_gain.reshape(1, d_model), freq, positions, w_query, w_key, w_value, w_out,
            k_cache.reshape(flat), v_cache.reshape(flat),
        )
        any_space = pl.BlockSpec(memory_space=pl.ANY)
        return pl.pallas_call(
            functools.partial(update_kernel, None),
            out_shape=[
                jax.ShapeDtypeStruct(hidden.shape, BF16),
                jax.ShapeDtypeStruct(k_cache.shape, BF16),
                jax.ShapeDtypeStruct(v_cache.shape, BF16),
            ],
            in_specs=[vmem] * 5 + [pl.BlockSpec(memory_space=pltpu.SMEM)],
            out_specs=[vmem, any_space, any_space],
            scratch_shapes=[dma((2, batch)), dma((2,))],
            compiler_params=pltpu.CompilerParams(vmem_limit_bytes=16 << 20),
            cost_estimate=pl.CostEstimate(flops=1_000_000, bytes_accessed=8_000_000, transcendentals=0),
            name="cache_update",
        )(y, k_cache, v_cache, k_new, v_new, positions)

    cache_spec = P("dp", "sp", "tp", None)
    specs_in = (P("dp", None), P(None), P(None, "tp"), P(None, "tp"), P(None, "tp"), P("tp", None), cache_spec, cache_spec, P("dp"))
    specs_out = (P("dp", None), cache_spec, cache_spec)
    return jax.shard_map(local_step, mesh=mesh, in_specs=specs_in, out_specs=specs_out, check_vma=False)
```

time: 210 us -> 51.8 us (0.25)
  waiting for transfers between devices: 105 us -> 0 us
  matrix products: 56.5 us -> 0 us
  Pallas kernels: 0 us -> 37.9 us
  other arithmetic: 27.8 us -> 0 us
  between operations: 14.1 us -> 0.66 us
  local copies, waits for them, and re-layouts: 5.69 us -> 12.8 us
    all_gather x1 -> x0, waiting for transfers between devices: 80.9 us -> none  [local_step(): gathered = lax.all_gather(block_stats, 'sp')]
    dot_general x6 -> x0, matrix products: 56.5 us -> none  [the longest x1 23.3 us: local_step(): part_proj = jnp.dot(attn_out, w_out, preferred_element_type=jnp.float32)]
    pallas_call x0 -> x2, Pallas kernels: none -> 37.9 us  [the longest x1 34.6 us: local_step(): pl.pallas_call(attention_kernel, out_shape=[jax.ShapeDtypeStruct(hidden.s...]
    psum x1 -> x0, waiting for transfers between devices: 23.7 us -> none  [local_step(): proj_out = lax.psum(part_proj, 'tp')]
    unnamed x9 -> x16, local copies, waits for them, and re-layouts: 1.32 us -> 12.8 us
    reduce_sum x4 -> x0, other arithmetic: 10.8 us -> none  [the longest x1 6.65 us: local_step(): total_sum = jnp.sum(gathered[..., head_dim:head_dim + 1] * rescale, axis=0)]
    select_n x1 -> x0, other arithmetic: 9.43 us -> none  [local_step(): v_updated = jnp.where(slot_mask, v_new[:, None], v_cache)]
    exp x1 -> x0, local copies, waits for them, and re-layouts: 3.67 us -> none  [local_step(): rescale = jnp.exp(all_max - global_max)]
  transfers between devices with their start and end apart: 2 -> 0, of which waited for: 2 -> 0; matrix products, arithmetic and copies ran while one was open for 0% -> 0% of each run, Pallas kernels for 0% -> 0%
where the time goes in v1:
time: 51.8 us; the launch traced here: 51.4 us
  Pallas kernels  37.9 us (73%)
  local copies, waits for them, and re-layouts  12.8 us (25%)
  between operations  0.66 us (1%)
    pallas_call x1, Pallas kernels, local_step(): pl.pallas_call(attention_kernel, out_shape=[jax.ShapeDtypeStruct(hidden.s...  34.6 us
    unnamed x16, local copies, waits for them, and re-layouts  12.8 us
    pallas_call x1, Pallas kernels, local_step(): pl.pallas_call(functools.partial(update_kernel, None), out_shape=[jax.Sha...  3.26 us

profile of v1, /device:TPU:1, one launch (start us, length us, event | category | flops | bytes accessed | tf_op | source)
XLA Modules:
  0.0 51.4 jit_solution(6387508810555397771)
XLA Ops:
  0.6 0.0 copy-start
  0.6 1.6 %copy-done = bf16[4,512,4,128]{3,2,1,0:T(4,128)(2,1)S(1)} copy-done((bf16[4,512,4,128]{3,2,1,0:T(4,128)(2,1)S(1)}, bf16[4,512,4,128]{3,2,1,0:T(4,128)(2,1)}, u32[]{:S(2)}) %copy-start) | copy-done | bytes 2097176
  2.2 0.0 copy-start.1
  2.2 1.6 %copy-done.1 = bf16[4,512,4,128]{3,2,1,0:T(4,128)(2,1)S(1)} copy-done((bf16[4,512,4,128]{3,2,1,0:T(4,128)(2,1)S(1)}, bf16[4,512,4,128]{3,2,1,0:T(4,128)(2,1)}, u32[]{:S(2)}) %copy-start.1) | copy-done | bytes 2097176
  3.8 0.0 copy-start.2
  3.8 3.4 %copy-done.2 = bf16[8192,512]{1,0:T(8,128)(2,1)S(1)} copy-done((bf16[8192,512]{1,0:T(8,128)(2,1)S(1)}, bf16[8192,512]{1,0:T(8,128)(2,1)}, u32[]{:S(2)}) %copy-start.2) | copy-done | bytes 8388632
  7.2 0.0 copy-start.3
  7.2 3.4 %copy-done.3 = bf16[8192,512]{1,0:T(8,128)(2,1)S(1)} copy-done((bf16[8192,512]{1,0:T(8,128)(2,1)S(1)}, bf16[8192,512]{1,0:T(8,128)(2,1)}, u32[]{:S(2)}) %copy-start.3) | copy-done | bytes 8388632
  10.6 0.0 copy-start.4
  10.6 0.8 %copy-done.4 = bf16[4,8192]{1,0:T(4,128)(2,1)S(1)} copy-done((bf16[4,8192]{1,0:T(4,128)(2,1)S(1)}, bf16[4,8192]{1,0:T(4,128)(2,1)}, u32[]{:S(2)}) %copy-start.4) | copy-done | bytes 65560
  11.4 0.0 copy-start.5
  11.4 0.8 %copy-done.5 = f32[8192]{0:T(1024)S(1)} copy-done((f32[8192]{0:T(1024)S(1)}, f32[8192]{0:T(1024)}, u32[]{:S(2)}) %copy-start.5) | copy-done | bytes 32792
  12.2 0.0 copy-start.6
  12.2 0.7 %copy-done.6 = s32[4]{0:T(128)S(1)} copy-done((s32[4]{0:T(128)S(1)}, s32[4]{0:T(128)}, u32[]{:S(2)}) %copy-start.6) | copy-done | bytes 40
  12.8 0.0 copy-start.7
  12.8 0.7 %copy-done.7 = f32[1,128]{1,0:T(1,128)S(1)} copy-done((f32[1,128]{1,0:T(1,128)S(1)}, f32[1,128]{1,0:T(1,128)}, u32[]{:S(2)}) %copy-start.7) | copy-done | bytes 536
  13.5 34.6 %attention_step.1 = (bf16[4,8192]{1,0:T(4,128)(2,1)S(1)}, bf16[4,4,128]{2,1,0:T(4,128)(2,1)S(1)}, bf16[4,4,128]{2,1,0:T(4,128)(2,1)S(1)}) custom-call(bf16[4,8192]{1,0:T(4,128)(2,1)S(1)} %copy-done.4, f32[1,8192]{1,0:T(1,128)S(1)} %bitcast.5, f32[1,128]{1,0:T(1,128)S(1)} %copy-done.7, s32[4]{0:T(128)S(1)} %copy-done.6, bf16[8192,4096]{1,0:T(8,128)(2,1)} %wq_hbm.1, ...), custom_call_target="tpu_custom_call" | custom-call | flops 20000000000 | bytes 20000000 | tf_op jit(solution)/shard_map/attention_step/pallas_call | solution.py:311
  48.1 3.3 %cache_update.1 = (bf16[4,8192]{1,0:T(4,128)(2,1)}, bf16[4,512,4,128]{3,2,1,0:T(4,128)(2,1)}, bf16[4,512,4,128]{3,2,1,0:T(4,128)(2,1)}) custom-call(bf16[4,8192]{1,0:T(4,128)(2,1)S(1)} %get-tuple-element.6.y_ref, bf16[4,512,4,128]{3,2,1,0:T(4,128)(2,1)S(1)} %copy-done, bf16[4,512,4,128]{3,2,1,0:T(4,128)(2,1)S(1)} %copy-done.1, ...), custom_call_target="tpu_custom_call" | custom-call | flops 1000000 | bytes 8000000 | tf_op jit(solution)/shard_map/cache_update/pallas_call | solution.py:355
Async XLA Ops:
  0.6 1.6 %copy-start = (bf16[4,512,4,128]{3,2,1,0:T(4,128)(2,1)S(1)}, bf16[4,512,4,128]{3,2,1,0:T(4,128)(2,1)}, u32[]{:S(2)}) copy-start(bf16[4,512,4,128]{3,2,1,0:T(4,128)(2,1)} %k_ref.1) | copy-start | bytes 6291460
  2.2 1.6 %copy-start.1 = (bf16[4,512,4,128]{3,2,1,0:T(4,128)(2,1)S(1)}, bf16[4,512,4,128]{3,2,1,0:T(4,128)(2,1)}, u32[]{:S(2)}) copy-start(bf16[4,512,4,128]{3,2,1,0:T(4,128)(2,1)} %v_ref.1) | copy-start | bytes 6291460
  3.8 3.4 %copy-start.2 = (bf16[8192,512]{1,0:T(8,128)(2,1)S(1)}, bf16[8192,512]{1,0:T(8,128)(2,1)}, u32[]{:S(2)}) copy-start(bf16[8192,512]{1,0:T(8,128)(2,1)} %wk_hbm.1) | copy-start | bytes 25165828
  7.2 3.4 %copy-start.3 = (bf16[8192,512]{1,0:T(8,128)(2,1)S(1)}, bf16[8192,512]{1,0:T(8,128)(2,1)}, u32[]{:S(2)}) copy-start(bf16[8192,512]{1,0:T(8,128)(2,1)} %wv_hbm.1) | copy-start | bytes 25165828
  10.6 0.8 %copy-start.4 = (bf16[4,8192]{1,0:T(4,128)(2,1)S(1)}, bf16[4,8192]{1,0:T(4,128)(2,1)}, u32[]{:S(2)}) copy-start(bf16[4,8192]{1,0:T(4,128)(2,1)} %hidden_hbm.1) | copy-start | bytes 196612
  11.4 0.8 %copy-start.5 = (f32[8192]{0:T(1024)S(1)}, f32[8192]{0:T(1024)}, u32[]{:S(2)}) copy-start(f32[8192]{0:T(1024)} %param.11) | copy-start | bytes 98308
  12.2 0.7 %copy-start.6 = (s32[4]{0:T(128)S(1)}, s32[4]{0:T(128)}, u32[]{:S(2)}) copy-start(s32[4]{0:T(128)} %pos_ref.1) | copy-start | bytes 52
  12.8 0.7 %copy-start.7 = (f32[1,128]{1,0:T(1,128)S(1)}, f32[1,128]{1,0:T(1,128)}, u32[]{:S(2)}) copy-start(f32[1,128]{1,0:T(1,128)} %constant.2.clone.freq_hbm) | copy-start | bytes 1540

commit v2 on v1

v2 whole, which is shorter than its diff:
```python
import jax
import jax.numpy as jnp
import numpy as np
from jax import lax
from jax.experimental import pallas as pl
from jax.experimental.pallas import tpu as pltpu
from jax.sharding import PartitionSpec as P

ROPE_BASE = 1000000.0
EPS = 1e-5
NEG_BIG = -3.0e38
SIDE = 4
PLANE = SIDE * SIDE
AXES = ("x", "y", "z")
PARTS = ((0, 24, True), (1, 24, True), (2, 24, True), (0, 24, False), (1, 16, False), (2, 16, False))
STARTS = tuple(sum(d for _, d, _ in PARTS[:i]) for i in range(len(PARTS)))
HALVES = 2
CHUNKS = 8
BF16 = jnp.bfloat16
F32 = jnp.float32


def sum_bytes(ref, sem):
    pltpu.make_async_copy(ref, ref, sem).wait()


def attention_kernel(
    hidden_hbm, gain_hbm, freq_hbm, pos_hbm, wq_hbm, wk_hbm, wv_hbm, wo_hbm, k_hbm, v_hbm,
    out_ref, knew_ref, vnew_ref,
    hid, gain, freq, wq, wk, wv, wo, kbuf, vbuf, kturn, gathered, fresh, rows, x0, x1, x2, x3, x4, x5, orow,
    ypart, ypeer, yall, pos, sems, wq_sems, part_send, part_recv, qsend, qrecv, tpsend, tprecv, ysend, yrecv,
):
    batch, d_model = hid.shape
    head = 128
    seq_local = kbuf.shape[1] // 4
    me = lax.axis_index("sp")
    core = lax.axis_index("tp")
    lx = lax.rem(me, SIDE)
    ly = lax.rem(me // SIDE, SIDE)
    lz = me // PLANE
    cell = lax.rem(me, PLANE)
    line = {"x": lx, "y": ly, "z": lz}
    stride = {"x": 1, "y": SIDE, "z": PLANE}

    def line_peer(axis, step):
        here = line[axis]
        return me + (lax.rem(here + step, SIDE) - here) * stride[axis]

    def plane_peer(step_y, step_x):
        return lz * PLANE + lax.rem(ly + step_y, SIDE) * SIDE + lax.rem(lx + step_x, SIDE)

    plane_steps = sorted(
        [(a, b) for a in range(SIDE) for b in range(SIDE) if (a, b) != (0, 0)],
        key=lambda s: -(min(s[0], SIDE - s[0]) + min(s[1], SIDE - s[1])),
    )

    cp_hid = pltpu.make_async_copy(hidden_hbm, hid, sems.at[0])
    cp_gain = pltpu.make_async_copy(gain_hbm, gain, sems.at[1])
    cp_pos = pltpu.make_async_copy(pos_hbm, pos, sems.at[2])
    cp_freq = pltpu.make_async_copy(freq_hbm, freq, sems.at[3])
    for cp in (cp_hid, cp_gain, cp_pos, cp_freq):
        cp.start()
    q_cols = pl.ds(pl.multiple_of(cell * 256, 256), 256)
    q_rows = d_model // CHUNKS
    cp_wq = [
        pltpu.make_async_copy(
            wq_hbm.at[pl.ds(c * q_rows, q_rows), q_cols], wq.at[pl.ds(c * q_rows, q_rows), :], wq_sems.at[c]
        )
        for c in range(CHUNKS)
    ]
    kv_depth = d_model // SIDE
    kv_rows = pl.ds(pl.multiple_of(lx * kv_depth, kv_depth), kv_depth)
    kv_cols = pl.ds(pl.multiple_of(ly * head, head), head)
    cp_wk = pltpu.make_async_copy(wk_hbm.at[kv_rows, kv_cols], wk, sems.at[4])
    cp_wv = pltpu.make_async_copy(wv_hbm.at[kv_rows, kv_cols], wv, sems.at[5])
    cp_wk.start()
    cp_wv.start()
    for cp in cp_wq:
        cp.start()
    cp_k = pltpu.make_async_copy(k_hbm, kbuf, sems.at[6])
    cp_v = pltpu.make_async_copy(v_hbm, vbuf, sems.at[7])
    n_cols = wo.shape[1]
    o_cols = pl.ds(pl.multiple_of(cell * n_cols, n_cols), n_cols)
    cp_wo = pltpu.make_async_copy(wo_hbm.at[:, o_cols], wo, sems.at[8])

    barrier = pltpu.get_barrier_semaphore()
    for a, b in plane_steps:
        pl.semaphore_signal(barrier, inc=1, device_id={"sp": plane_peer(a, b), "tp": core})
    for step in (2, 1, 3):
        pl.semaphore_signal(barrier, inc=1, device_id={"sp": line_peer("z", step), "tp": core})
    pl.semaphore_signal(barrier, inc=1, device_id={"sp": me, "tp": 1 - core})

    cp_hid.wait()
    cp_gain.wait()
    resid = hid[...].astype(F32)
    scale = lax.rsqrt(jnp.mean(resid * resid, axis=-1, keepdims=True) + EPS)
    normed = (resid * scale * gain[...]).astype(BF16)

    rows[...] = normed.astype(F32)
    normed_kv = rows[:, kv_rows].astype(BF16)
    cp_wk.wait()
    cp_wv.wait()
    k_part = jnp.dot(normed_kv, wk[...], preferred_element_type=F32)
    v_part = jnp.dot(normed_kv, wv[...], preferred_element_type=F32)
    q_acc = jnp.zeros((batch, 256), F32)
    for c in range(CHUNKS):
        if c == 2:
            cp_pos.wait()
            cp_freq.wait()
            row4 = lax.broadcasted_iota(jnp.int32, (batch, head), 0)
            lane4 = lax.broadcasted_iota(jnp.int32, (batch, head), 1)
            pos_rows = jnp.zeros((batch, head), jnp.int32)
            for b in range(batch):
                pos_rows = jnp.where(row4 == b, pos[b], pos_rows)
            angles = pos_rows.astype(F32) * freq[...]
            cosine = jnp.cos(angles)
            sine = jnp.sin(angles)
            sine = jnp.where(lane4 < head // 2, -sine, sine)
        cp_wq[c].wait()
        q_acc += jnp.dot(
            normed[:, c * q_rows:(c + 1) * q_rows], wq[c * q_rows:(c + 1) * q_rows, :], preferred_element_type=F32
        )
    cp_k.start()
    cp_v.start()

    def rotate(u):
        return u * cosine + pltpu.roll(u, head // 2, axis=1) * sine

    q_lo = rotate(q_acc[:, :head]).astype(BF16).astype(F32)
    q_hi = rotate(q_acc[:, head:]).astype(BF16).astype(F32)
    mine = pl.ds(pl.multiple_of(cell * 16, 16), 16)
    gathered[mine, :] = jnp.concatenate([q_lo, q_hi, k_part, v_part], axis=0)

    pl.semaphore_wait(barrier, PLANE - 1 + SIDE - 1 + 1)
    for a, b in plane_steps:
        pltpu.make_async_remote_copy(
            src_ref=gathered.at[mine], dst_ref=gathered.at[mine], send_sem=qsend, recv_sem=qrecv,
            device_id={"sp": plane_peer(a, b), "tp": core},
        ).start()
    cp_wo.start()
    cp_k.wait()
    for b in range(batch):
        kturn[b] = kbuf[b].T
    sum_bytes(gathered.at[pl.ds(0, 16 * (PLANE - 1))], qrecv)

    cos_all = jnp.concatenate([cosine] * 4, axis=0)
    sin_all = jnp.concatenate([sine] * 4, axis=0)
    k_sum, v_sum = [], []
    for j in range(4):
        k_sum.append(sum(gathered[(4 * j + i) * 16 + 8:(4 * j + i) * 16 + 12, :] for i in range(4)))
        v_sum.append(sum(gathered[(4 * j + i) * 16 + 12:(4 * j + i) * 16 + 16, :] for i in range(4)))
    k_all = jnp.concatenate(k_sum, axis=0)
    v_all = jnp.concatenate(v_sum, axis=0)
    k_all = k_all * cos_all + pltpu.roll(k_all, head // 2, axis=1) * sin_all
    fresh[0:16, :] = k_all.astype(BF16).astype(F32)
    fresh[16:32, :] = v_all.astype(BF16).astype(F32)

    cols = seq_local * 4
    row_head = lax.rem(lax.broadcasted_iota(jnp.int32, (32, cols), 0), 16) // 4
    col_id = lax.broadcasted_iota(jnp.int32, (32, cols), 1)
    same_head = row_head == lax.rem(col_id, 4)
    new_row = lax.rem(lax.broadcasted_iota(jnp.int32, (32, 16), 0), 16) // 4
    new_head = new_row == lax.broadcasted_iota(jnp.int32, (32, 16), 1)
    ones16 = lax.broadcasted_iota(jnp.int32, (32, 16), 1) * 0
    base = me * seq_local
    pad = jnp.zeros((12, head), F32)
    dims_last = (((1,), (1,)), ((), ()))
    cp_v.wait()
    acc_rows, m_rows, l_rows = [], [], []
    for b in range(batch):
        k_b = jnp.concatenate([fresh[pl.ds(b, 4, stride=4), :], pad], axis=0).astype(BF16)
        v_b = jnp.concatenate([fresh[pl.ds(16 + b, 4, stride=4), :], pad], axis=0).astype(BF16)
        knew_ref[b, 0] = k_b[0:4]
        vnew_ref[b, 0] = v_b[0:4]
        q_b = jnp.concatenate(
            [gathered[pl.ds(b, 16, stride=16), :], gathered[pl.ds(4 + b, 16, stride=16), :]], axis=0
        ).astype(BF16)
        limit = (pos[b] - base) * 4
        valid = jnp.logical_and(same_head, col_id < limit)
        valid_new = jnp.logical_and(
            new_head, jnp.logical_and(ones16 + limit >= 0, ones16 + limit < cols)
        )
        s = jnp.dot(q_b, kturn[b], preferred_element_type=F32) * (head ** -0.5)
        s_new = lax.dot_general(q_b, k_b, dims_last, preferred_element_type=F32) * (head ** -0.5)
        s = jnp.where(valid, s, NEG_BIG)
        s_new = jnp.where(valid_new, s_new, NEG_BIG)
        m = jnp.maximum(jnp.max(s, axis=-1, keepdims=True), jnp.max(s_new, axis=-1, keepdims=True))
        p = jnp.where(valid, jnp.exp(s - m), 0.0)
        p_new = jnp.where(valid_new, jnp.exp(s_new - m), 0.0)
        l_rows.append(jnp.sum(p, axis=-1, keepdims=True) + jnp.sum(p_new, axis=-1, keepdims=True))
        m_rows.append(m)
        acc_rows.append(
            jnp.dot(p.astype(BF16), vbuf[b], preferred_element_type=F32)
            + jnp.dot(p_new.astype(BF16), v_b, preferred_element_type=F32)
        )
    acc_t = jnp.concatenate(acc_rows, axis=0).T
    m_col = jnp.concatenate(m_rows, axis=0)
    l_col = jnp.concatenate(l_rows, axis=0)
    lane = lax.broadcasted_iota(jnp.int32, (128, 128), 1)
    stat_t = jnp.where(lane == 0, m_col, l_col).T[0:8]

    parts = (x0, x1, x2, x3, x4, x5)

    def send_part(p, t):
        axis = AXES[(PARTS[p][0] + t) % 3]
        slot = parts[p].at[t, line[axis]]
        for step in (2, 1, 3):
            pltpu.make_async_remote_copy(
                src_ref=slot, dst_ref=slot, send_sem=part_send.at[p, t], recv_sem=part_recv.at[p, t],
                device_id={"sp": line_peer(axis, step), "tp": core},
            ).start()

    for p, (order, dims, has_stats) in enumerate(PARTS):
        slot = line[AXES[order]]
        parts[p][0, slot, 0:dims, :] = acc_t[STARTS[p]:STARTS[p] + dims]
        if has_stats:
            parts[p][0, slot, dims:dims + 8, :] = stat_t
        send_part(p, 0)
    o_parts = []
    row8 = lax.broadcasted_iota(jnp.int32, (8, 128), 0)
    factors = {}
    for t in range(3):
        for p, (order, dims, has_stats) in enumerate(PARTS):
            ref = parts[p]
            sum_bytes(ref.at[t, pl.ds(0, SIDE - 1)], part_recv.at[p, t])
            if has_stats:
                stats = [ref[t, i, dims:dims + 8, :] for i in range(SIDE)]
                ms = [st[0:1] for st in stats]
                top = jnp.maximum(jnp.maximum(ms[0], ms[1]), jnp.maximum(ms[2], ms[3]))
                fac = [jnp.exp(mi - top) for mi in ms]
                total = sum(stats[i][1:2] * fac[i] for i in range(SIDE))
                factors[order] = (fac, total)
            fac, total = factors[order]
            acc = sum(ref[t, i, 0:dims, :] * fac[i] for i in range(SIDE))
            if t < 2:
                slot = line[AXES[(order + t + 1) % 3]]
                ref[t + 1, slot, 0:dims, :] = acc
                if has_stats:
                    ref[t + 1, slot, dims:dims + 8, :] = jnp.where(row8 == 0, top, total)
                send_part(p, t + 1)
            else:
                o_parts.append(acc / total)
    orow[...] = jnp.concatenate(o_parts, axis=0).T

    attn = jnp.concatenate(
        [orow[pl.ds(h // 2 + 16 * (h % 2), batch, stride=32), :] for h in range(32)], axis=1
    ).astype(BF16)
    cp_wo.wait()
    o_rows = wo.shape[0] // CHUNKS
    half = n_cols // HALVES
    cp_tp = []
    for u in range(HALVES):
        y = jnp.zeros((batch, half), F32)
        for c in range(CHUNKS):
            y += jnp.dot(
                attn[:, c * o_rows:(c + 1) * o_rows],
                wo[c * o_rows:(c + 1) * o_rows, u * half:(u + 1) * half],
                preferred_element_type=F32,
            )
        ypart[u] = y
        cp_tp.append(
            pltpu.make_async_remote_copy(
                src_ref=ypart.at[u], dst_ref=ypeer.at[u], send_sem=tpsend.at[u], recv_sem=tprecv.at[u],
                device_id={"sp": me, "tp": 1 - core},
            )
        )
        cp_tp[u].start()
    for u in range(HALVES):
        cp_tp[u].wait_recv()
        yall[u, cell] = ypart[u] + ypeer[u]
        for a, b in plane_steps:
            pltpu.make_async_remote_copy(
                src_ref=yall.at[u, cell], dst_ref=yall.at[u, cell], send_sem=ysend.at[u], recv_sem=yrecv.at[u],
                device_id={"sp": plane_peer(a, b), "tp": core},
            ).start()

    sum_bytes(gathered.at[pl.ds(0, 16 * (PLANE - 1))], qsend)
    for t in range(3):
        for p in range(len(PARTS)):
            sum_bytes(parts[p].at[t, pl.ds(0, SIDE - 1)], part_send.at[p, t])
    for u in range(HALVES):
        cp_tp[u].wait_send()

    for u in range(HALVES):
        sum_bytes(yall.at[u, pl.ds(0, PLANE - 1)], yrecv.at[u])
        for i in range(PLANE):
            lo = i * n_cols + u * half
            out_ref[:, lo:lo + half] = (hid[:, lo:lo + half].astype(F32) + yall[u, i]).astype(BF16)
    for u in range(HALVES):
        sum_bytes(yall.at[u, pl.ds(0, PLANE - 1)], ysend.at[u])


def update_kernel(y_ref, k_ref, v_ref, knew_ref, vnew_ref, pos_ref, out_ref, ko_ref, vo_ref, y_sem, sems):
    batch, seq_local = k_ref.shape[0], k_ref.shape[1]
    base = lax.axis_index("sp") * seq_local
    copies = [pltpu.make_async_copy(y_ref, out_ref, y_sem)]
    for b in range(batch):
        spot = pos_ref[b] - base
        here = jnp.logical_and(spot >= 0, spot < seq_local).astype(jnp.int32)
        before = here * spot + (1 - here) * seq_local
        spot = here * spot
        after = here * (seq_local - 1 - spot)
        tail = pl.ds(seq_local - after, after)
        for i, (src, new, dst) in enumerate(((k_ref, knew_ref, ko_ref), (v_ref, vnew_ref, vo_ref))):
            head_rows = pl.ds(0, before)
            row = pl.ds(spot, here)
            copies.append(pltpu.make_async_copy(src.at[b, head_rows], dst.at[b, head_rows], sems.at[i, b, 0]))
            copies.append(pltpu.make_async_copy(src.at[b, tail], dst.at[b, tail], sems.at[i, b, 1]))
            copies.append(pltpu.make_async_copy(new.at[b, pl.ds(0, here)], dst.at[b, row], sems.at[i, b, 2]))
    for cp in copies:
        cp.start()
    for cp in copies:
        cp.wait()


def solution(mesh):
    def local_step(hidden, norm_gain, w_query, w_key, w_value, w_out, k_cache, v_cache, positions):
        batch, seq_local, kv_local, head = k_cache.shape
        d_model = hidden.shape[1]
        n_cols = w_out.shape[1] // PLANE
        half = np.arange(head // 2, dtype=np.float32) * np.float32(2.0) / np.float32(head)
        inv = (np.float32(1.0) / np.power(np.float32(ROPE_BASE), half)).astype(np.float32)
        freq = jnp.asarray(np.concatenate([inv, inv])[None, :])
        flat = (batch, seq_local * kv_local, head)
        hbm = pl.BlockSpec(memory_space=pltpu.HBM)
        vmem = pl.BlockSpec(memory_space=pltpu.VMEM)
        dma = pltpu.SemaphoreType.DMA
        y, k_new, v_new = pl.pallas_call(
            attention_kernel,
            out_shape=[
                jax.ShapeDtypeStruct(hidden.shape, BF16),
                jax.ShapeDtypeStruct((batch, 1, kv_local, head), BF16),
                jax.ShapeDtypeStruct((batch, 1, kv_local, head), BF16),
            ],
            in_specs=[hbm] * 10,
            out_specs=[vmem] * 3,
            scratch_shapes=[
                pltpu.VMEM(hidden.shape, BF16),
                pltpu.VMEM((1, d_model), F32),
                pltpu.VMEM((1, head), F32),
                pltpu.VMEM((d_model, 256), BF16),
                pltpu.VMEM((d_model // SIDE, head), BF16),
                pltpu.VMEM((d_model // SIDE, head), BF16),
                pltpu.VMEM((w_out.shape[0], n_cols), BF16),
                pltpu.VMEM(flat, BF16),
                pltpu.VMEM(flat, BF16),
                pltpu.VMEM((batch, head, seq_local * kv_local), BF16),
                pltpu.VMEM((PLANE * 16, head), F32),
                pltpu.VMEM((32, head), F32),
                pltpu.VMEM((batch, d_model), F32),
                *[pltpu.VMEM((3, SIDE, d + 8 * stats, 128), F32) for _, d, stats in PARTS],
                pltpu.VMEM((128, 128), F32),
                pltpu.VMEM((HALVES, batch, n_cols // HALVES), F32),
                pltpu.VMEM((HALVES, batch, n_cols // HALVES), F32),
                pltpu.VMEM((HALVES, PLANE, batch, n_cols // HALVES), F32),
                pltpu.SMEM((batch,), jnp.int32),
                dma((9,)),
                dma((CHUNKS,)),
                dma((len(PARTS), 3)),
                dma((len(PARTS), 3)),
                dma, dma,
                *[dma((HALVES,))] * 4,
            ],
            compiler_params=pltpu.CompilerParams(
                collective_id=0, has_side_effects=True, vmem_limit_bytes=30 << 20
            ),
            cost_estimate=pl.CostEstimate(flops=20_000_000_000, bytes_accessed=20_000_000, transcendentals=0),
            name="attention_step",
        )(
            *[
                pltpu.with_memory_space_constraint(a, pltpu.HBM)
                for a in (
                    hidden, norm_gain.reshape(1, d_model), freq, positions, w_query, w_key, w_value, w_out,
                    k_cache.reshape(flat), v_cache.reshape(flat),
                )
            ]
        )
        any_space = pl.BlockSpec(memory_space=pl.ANY)
        return pl.pallas_call(
            update_kernel,
            out_shape=[
                jax.ShapeDtypeStruct(hidden.shape, BF16),
                jax.ShapeDtypeStruct(k_cache.shape, BF16),
                jax.ShapeDtypeStruct(v_cache.shape, BF16),
            ],
            in_specs=[vmem] * 5 + [pl.BlockSpec(memory_space=pltpu.SMEM)],
            out_specs=[any_space] * 3,
            scratch_shapes=[dma, dma((2, batch, 3))],
            compiler_params=pltpu.CompilerParams(vmem_limit_bytes=16 << 20),
            cost_estimate=pl.CostEstimate(flops=1_000_000, bytes_accessed=8_000_000, transcendentals=0),
            name="cache_update",
        )(y, k_cache, v_cache, k_new, v_new, positions)

    cache_spec = P("dp", "sp", "tp", None)
    specs_in = (P("dp", None), P(None), P(None, "tp"), P(None, "tp"), P(None, "tp"), P("tp", None), cache_spec, cache_spec, P("dp"))
    specs_out = (P("dp", None), cache_spec, cache_spec)
    return jax.shard_map(local_step, mesh=mesh, in_specs=specs_in, out_specs=specs_out, check_vma=False)
```

time: 51.8 us -> 39.1 us (0.75)
  local copies, waits for them, and re-layouts: 12.8 us -> 0.01 us
    unnamed x16 -> x6, local copies, waits for them, and re-layouts: 12.8 us -> 0.01 us
    pallas_call x1, Pallas kernels: 34.6 us -> 35.4 us  [local_step(): pl.pallas_call(attention_kernel, out_shape=[jax.ShapeDtypeStruct(hidden.s...]
where the time goes in v2:
time: 39.1 us; the launch traced here: 39 us
  Pallas kernels  38.3 us (98%)
  between operations  0.69 us (2%)
    pallas_call x1, Pallas kernels, local_step(): pl.pallas_call(attention_kernel, out_shape=[jax.ShapeDtypeStruct(hidden.s...  35.4 us
    pallas_call x1, Pallas kernels, local_step(): pl.pallas_call(update_kernel, out_shape=[jax.ShapeDtypeStruct(hidden.shap...  2.88 us

profile of v2, /device:TPU:1, one launch (start us, length us, event | category | flops | bytes accessed | tf_op | source)
XLA Modules:
  0.0 39.0 jit_solution(6032707107071225588)
XLA Ops:
  0.6 0.0 copy-start
  0.6 0.0 copy-start.1
  0.7 0.0 copy-start.2
  0.7 35.4 %attention_step.1 = (bf16[4,8192]{1,0:T(4,128)(2,1)S(1)}, bf16[4,1,4,128]{3,2,1,0:T(4,128)(2,1)S(1)}, bf16[4,1,4,128]{3,2,1,0:T(4,128)(2,1)S(1)}) custom-call(bf16[4,8192]{1,0:T(4,128)(2,1)} %hidden_hbm.1, f32[1,8192]{1,0:T(1,128)} %bitcast.5, f32[1,128]{1,0:T(1,128)} %constant.2.clone.freq_hbm, s32[4]{0:T(128)} %pos_ref.1, bf16[8192,4096]{1,0:T(8,128)(2,1)} %wq_hbm.1, ...), custom_call_target="tpu_custom_call" | custom-call | flops 20000000000 | bytes 20000000 | tf_op jit(solution)/shard_map/attention_step/pallas_call | solution.py:328
  36.1 0.0 copy-done
  36.1 0.0 copy-done.1
  36.1 0.0 copy-done.2
  36.1 2.9 %cache_update.1 = (bf16[4,8192]{1,0:T(4,128)(2,1)}, bf16[4,512,4,128]{3,2,1,0:T(4,128)(2,1)}, bf16[4,512,4,128]{3,2,1,0:T(4,128)(2,1)}) custom-call(bf16[4,8192]{1,0:T(4,128)(2,1)S(1)} %get-tuple-element.6.y_ref, bf16[4,512,4,128]{3,2,1,0:T(4,128)(2,1)S(1)} %copy-done, bf16[4,512,4,128]{3,2,1,0:T(4,128)(2,1)S(1)} %copy-done.1, ...), custom_call_target="tpu_custom_call" | custom-call | flops 1000000 | bytes 8000000 | tf_op jit(solution)/shard_map/cache_update/pallas_call | solution.py:379
Async XLA Ops:
  0.6 35.4 %copy-start = (bf16[4,512,4,128]{3,2,1,0:T(4,128)(2,1)S(1)}, bf16[4,512,4,128]{3,2,1,0:T(4,128)(2,1)}, u32[]{:S(2)}) copy-start(bf16[4,512,4,128]{3,2,1,0:T(4,128)(2,1)} %k_ref.1) | copy-start | bytes 6291460
  0.6 35.4 %copy-start.1 = (bf16[4,512,4,128]{3,2,1,0:T(4,128)(2,1)S(1)}, bf16[4,512,4,128]{3,2,1,0:T(4,128)(2,1)}, u32[]{:S(2)}) copy-start(bf16[4,512,4,128]{3,2,1,0:T(4,128)(2,1)} %v_ref.1) | copy-start | bytes 6291460
  0.7 35.4 %copy-start.2 = (s32[4]{0:T(128)S(1)}, s32[4]{0:T(128)}, u32[]{:S(2)}) copy-start(s32[4]{0:T(128)} %pos_ref.1) | copy-start | bytes 52

commit v3 on v2

--- a/solution.py
+++ b/solution.py
@@ -12,7 +12,11 @@
 SIDE = 4
 PLANE = SIDE * SIDE
 AXES = ("x", "y", "z")
-PARTS = ((0, 24, True), (1, 24, True), (2, 24, True), (0, 24, False), (1, 16, False), (2, 16, False))
+PARTS = (
+    (0, 16, True), (1, 16, True), (2, 16, True),
+    (0, 16, False), (1, 16, False), (2, 16, False),
+    (0, 16, False), (1, 8, False), (2, 8, False),
+)
 STARTS = tuple(sum(d for _, d, _ in PARTS[:i]) for i in range(len(PARTS)))
 HALVES = 2
 CHUNKS = 8
@@ -26,8 +30,8 @@
 
 def attention_kernel(
     hidden_hbm, gain_hbm, freq_hbm, pos_hbm, wq_hbm, wk_hbm, wv_hbm, wo_hbm, k_hbm, v_hbm,
-    out_ref, knew_ref, vnew_ref,
-    hid, gain, freq, wq, wk, wv, wo, kbuf, vbuf, kturn, gathered, fresh, rows, x0, x1, x2, x3, x4, x5, orow,
+    out_ref, kbuf, vbuf,
+    hid, gain, freq, wq, wk, wv, wo, kturn, gathered, fresh, rows, x0, x1, x2, x3, x4, x5, x6, x7, x8, orow,
     ypart, ypeer, yall, pos, sems, wq_sems, part_send, part_recv, qsend, qrecv, tpsend, tprecv, ysend, yrecv,
 ):
     batch, d_model = hid.shape
@@ -102,7 +106,7 @@
     cp_wv.wait()
     k_part = jnp.dot(normed_kv, wk[...], preferred_element_type=F32)
     v_part = jnp.dot(normed_kv, wv[...], preferred_element_type=F32)
-    q_acc = jnp.zeros((batch, 256), F32)
+    q_acc = [jnp.zeros((batch, 256), F32), jnp.zeros((batch, 256), F32)]
     for c in range(CHUNKS):
         if c == 2:
             cp_pos.wait()
@@ -117,11 +121,13 @@
             sine = jnp.sin(angles)
             sine = jnp.where(lane4 < head // 2, -sine, sine)
         cp_wq[c].wait()
-        q_acc += jnp.dot(
-            normed[:, c * q_rows:(c + 1) * q_rows], wq[c * q_rows:(c + 1) * q_rows, :], preferred_element_type=F32
-        )
+        for u in range(2):
+            lo, hi = c * q_rows + u * q_rows // 2, c * q_rows + (u + 1) * q_rows // 2
+            q_acc[u] += jnp.dot(normed[:, lo:hi], wq[lo:hi, :], preferred_element_type=F32)
     cp_k.start()
     cp_v.start()
+
+    q_acc = q_acc[0] + q_acc[1]
 
     def rotate(u):
         return u * cosine + pltpu.roll(u, head // 2, axis=1) * sine
@@ -156,12 +162,14 @@
     fresh[16:32, :] = v_all.astype(BF16).astype(F32)
 
     cols = seq_local * 4
-    row_head = lax.rem(lax.broadcasted_iota(jnp.int32, (32, cols), 0), 16) // 4
-    col_id = lax.broadcasted_iota(jnp.int32, (32, cols), 1)
-    same_head = row_head == lax.rem(col_id, 4)
-    new_row = lax.rem(lax.broadcasted_iota(jnp.int32, (32, 16), 0), 16) // 4
-    new_head = new_row == lax.broadcasted_iota(jnp.int32, (32, 16), 1)
-    ones16 = lax.broadcasted_iota(jnp.int32, (32, 16), 1) * 0
+    tiles = cols // 128
+    lane = lax.broadcasted_iota(jnp.int32, (32, 128), 1)
+    row_head = (lax.broadcasted_iota(jnp.int32, (32, 128), 0) & 15) >> 2
+    column = jnp.where((lane & 3) == row_head, lane, 1 << 30)
+    new_row = (lax.broadcasted_iota(jnp.int32, (32, 16), 0) & 15) >> 2
+    new_lane = lax.broadcasted_iota(jnp.int32, (32, 16), 1)
+    new_head = new_row == new_lane
+    to_log2 = head ** -0.5 * 1.4426950408889634
     base = me * seq_local
     pad = jnp.zeros((12, head), F32)
     dims_last = (((1,), (1,)), ((), ()))
@@ -170,36 +178,50 @@
     for b in range(batch):
         k_b = jnp.concatenate([fresh[pl.ds(b, 4, stride=4), :], pad], axis=0).astype(BF16)
         v_b = jnp.concatenate([fresh[pl.ds(16 + b, 4, stride=4), :], pad], axis=0).astype(BF16)
-        knew_ref[b, 0] = k_b[0:4]
-        vnew_ref[b, 0] = v_b[0:4]
         q_b = jnp.concatenate(
             [gathered[pl.ds(b, 16, stride=16), :], gathered[pl.ds(4 + b, 16, stride=16), :]], axis=0
         ).astype(BF16)
         limit = (pos[b] - base) * 4
-        valid = jnp.logical_and(same_head, col_id < limit)
-        valid_new = jnp.logical_and(
-            new_head, jnp.logical_and(ones16 + limit >= 0, ones16 + limit < cols)
-        )
-        s = jnp.dot(q_b, kturn[b], preferred_element_type=F32) * (head ** -0.5)
-        s_new = lax.dot_general(q_b, k_b, dims_last, preferred_element_type=F32) * (head ** -0.5)
-        s = jnp.where(valid, s, NEG_BIG)
+        offset = new_lane * 0 + limit
+        valid_new = jnp.logical_and(new_head, jnp.logical_and(offset >= 0, offset < cols))
+        s_halves = [
+            jnp.dot(q_b, kturn[b, :, u * cols // 2:(u + 1) * cols // 2], preferred_element_type=F32) for u in range(2)
+        ]
+        s_new = lax.dot_general(q_b, k_b, dims_last, preferred_element_type=F32)
         s_new = jnp.where(valid_new, s_new, NEG_BIG)
-        m = jnp.maximum(jnp.max(s, axis=-1, keepdims=True), jnp.max(s_new, axis=-1, keepdims=True))
-        p = jnp.where(valid, jnp.exp(s - m), 0.0)
-        p_new = jnp.where(valid_new, jnp.exp(s_new - m), 0.0)
-        l_rows.append(jnp.sum(p, axis=-1, keepdims=True) + jnp.sum(p_new, axis=-1, keepdims=True))
+        s = []
+        for i in range(tiles):
+            u, j = divmod(i, tiles // 2)
+            s.append(jnp.where(column < limit - 128 * i, s_halves[u][:, 128 * j:128 * (j + 1)], NEG_BIG))
+        top = s
+        while len(top) > 1:
+            top = [jnp.maximum(top[i], top[i + 1]) for i in range(0, len(top), 2)]
+        m = jnp.maximum(jnp.max(top[0], axis=-1, keepdims=True), jnp.max(s_new, axis=-1, keepdims=True))
+        shift = jnp.where(m == NEG_BIG, 0.0, m)
+        p = [jnp.exp2((si - shift) * to_log2) for si in s]
+        p_new = jnp.exp2((s_new - shift) * to_log2)
+        total = p
+        while len(total) > 1:
+            total = [total[i] + total[i + 1] for i in range(0, len(total), 2)]
+        l_rows.append(jnp.sum(total[0], axis=-1, keepdims=True) + jnp.sum(p_new, axis=-1, keepdims=True))
         m_rows.append(m)
-        acc_rows.append(
-            jnp.dot(p.astype(BF16), vbuf[b], preferred_element_type=F32)
-            + jnp.dot(p_new.astype(BF16), v_b, preferred_element_type=F32)
-        )
+        half_tiles = tiles // 2
+        pv = [
+            jnp.dot(
+                jnp.concatenate([pi.astype(BF16) for pi in p[u * half_tiles:(u + 1) * half_tiles]], axis=1),
+                vbuf[b, u * cols // 2:(u + 1) * cols // 2, :],
+                preferred_element_type=F32,
+            )
+            for u in range(2)
+        ]
+        acc_rows.append(pv[0] + pv[1] + jnp.dot(p_new.astype(BF16), v_b, preferred_element_type=F32))
     acc_t = jnp.concatenate(acc_rows, axis=0).T
     m_col = jnp.concatenate(m_rows, axis=0)
     l_col = jnp.concatenate(l_rows, axis=0)
-    lane = lax.broadcasted_iota(jnp.int32, (128, 128), 1)
-    stat_t = jnp.where(lane == 0, m_col, l_col).T[0:8]
-
-    parts = (x0, x1, x2, x3, x4, x5)
+    stat_lane = lax.broadcasted_iota(jnp.int32, (128, 128), 1)
+    stat_t = jnp.where(stat_lane == 0, m_col, l_col).T[0:8]
+
+    parts = (x0, x1, x2, x3, x4, x5, x6, x7, x8)
 
     def send_part(p, t):
         axis = AXES[(PARTS[p][0] + t) % 3]
@@ -216,6 +238,24 @@
         if has_stats:
             parts[p][0, slot, dims:dims + 8, :] = stat_t
         send_part(p, 0)
+
+    tile_pos = lax.broadcasted_iota(jnp.int32, (16, head), 0) >> 2
+    block = 256
+    for buf, first in ((kbuf, 0), (vbuf, 16)):
+        for b in range(batch):
+            new4 = fresh[pl.ds(first + b, 4, stride=4), :]
+            new16 = jnp.concatenate([new4] * 4, axis=0).astype(BF16)
+            spot = pos[b] - base
+
+            def patch(i, carry, buf=buf, b=b, new16=new16, spot=spot):
+                for j in range(block // 16):
+                    at = pl.ds(pl.multiple_of(i * block + j * 16, 16), 16)
+                    hit = tile_pos == spot - i * (block // 4) - 4 * j
+                    buf[b, at, :] = jnp.where(hit, new16, buf[b, at, :])
+                return carry
+
+            lax.fori_loop(0, cols // block, patch, 0)
+
     o_parts = []
     row8 = lax.broadcasted_iota(jnp.int32, (8, 128), 0)
     factors = {}
@@ -227,7 +267,7 @@
                 stats = [ref[t, i, dims:dims + 8, :] for i in range(SIDE)]
                 ms = [st[0:1] for st in stats]
                 top = jnp.maximum(jnp.maximum(ms[0], ms[1]), jnp.maximum(ms[2], ms[3]))
-                fac = [jnp.exp(mi - top) for mi in ms]
+                fac = [jnp.exp2((mi - top) * to_log2) for mi in ms]
                 total = sum(stats[i][1:2] * fac[i] for i in range(SIDE))
                 factors[order] = (fac, total)
             fac, total = factors[order]
@@ -250,14 +290,14 @@
     half = n_cols // HALVES
     cp_tp = []
     for u in range(HALVES):
-        y = jnp.zeros((batch, half), F32)
+        y = [jnp.zeros((batch, half), F32), jnp.zeros((batch, half), F32)]
         for c in range(CHUNKS):
-            y += jnp.dot(
+            y[c % 2] += jnp.dot(
                 attn[:, c * o_rows:(c + 1) * o_rows],
                 wo[c * o_rows:(c + 1) * o_rows, u * half:(u + 1) * half],
                 preferred_element_type=F32,
             )
-        ypart[u] = y
+        ypart[u] = y[0] + y[1]
         cp_tp.append(
             pltpu.make_async_remote_copy(
                 src_ref=ypart.at[u], dst_ref=ypeer.at[u], send_sem=tpsend.at[u], recv_sem=tprecv.at[u],
@@ -290,23 +330,12 @@
         sum_bytes(yall.at[u, pl.ds(0, PLANE - 1)], ysend.at[u])
 
 
-def update_kernel(y_ref, k_ref, v_ref, knew_ref, vnew_ref, pos_ref, out_ref, ko_ref, vo_ref, y_sem, sems):
-    batch, seq_local = k_ref.shape[0], k_ref.shape[1]
-    base = lax.axis_index("sp") * seq_local
-    copies = [pltpu.make_async_copy(y_ref, out_ref, y_sem)]
-    for b in range(batch):
-        spot = pos_ref[b] - base
-        here = jnp.logical_and(spot >= 0, spot < seq_local).astype(jnp.int32)
-        before = here * spot + (1 - here) * seq_local
-        spot = here * spot
-        after = here * (seq_local - 1 - spot)
-        tail = pl.ds(seq_local - after, after)
-        for i, (src, new, dst) in enumerate(((k_ref, knew_ref, ko_ref), (v_ref, vnew_ref, vo_ref))):
-            head_rows = pl.ds(0, before)
-            row = pl.ds(spot, here)
-            copies.append(pltpu.make_async_copy(src.at[b, head_rows], dst.at[b, head_rows], sems.at[i, b, 0]))
-            copies.append(pltpu.make_async_copy(src.at[b, tail], dst.at[b, tail], sems.at[i, b, 1]))
-            copies.append(pltpu.make_async_copy(new.at[b, pl.ds(0, here)], dst.at[b, row], sems.at[i, b, 2]))
+def store_kernel(y_ref, k_ref, v_ref, out_ref, ko_ref, vo_ref, sems):
+    copies = []
+    for b in range(k_ref.shape[0]):
+        copies.append(pltpu.make_async_copy(k_ref.at[b], ko_ref.at[b], sems.at[2 * b]))
+        copies.append(pltpu.make_async_copy(v_ref.at[b], vo_ref.at[b], sems.at[2 * b + 1]))
+    copies.append(pltpu.make_async_copy(y_ref, out_ref, sems.at[2 * k_ref.shape[0]]))
     for cp in copies:
         cp.start()
     for cp in copies:
@@ -325,12 +354,12 @@
         hbm = pl.BlockSpec(memory_space=pltpu.HBM)
         vmem = pl.BlockSpec(memory_space=pltpu.VMEM)
         dma = pltpu.SemaphoreType.DMA
-        y, k_new, v_new = pl.pallas_call(
+        y, k_next, v_next = pl.pallas_call(
             attention_kernel,
             out_shape=[
                 jax.ShapeDtypeStruct(hidden.shape, BF16),
-                jax.ShapeDtypeStruct((batch, 1, kv_local, head), BF16),
-                jax.ShapeDtypeStruct((batch, 1, kv_local, head), BF16),
+                jax.ShapeDtypeStruct(flat, BF16),
+                jax.ShapeDtypeStruct(flat, BF16),
             ],
             in_specs=[hbm] * 10,
             out_specs=[vmem] * 3,
@@ -342,8 +371,6 @@
                 pltpu.VMEM((d_model // SIDE, head), BF16),
                 pltpu.VMEM((d_model // SIDE, head), BF16),
                 pltpu.VMEM((w_out.shape[0], n_cols), BF16),
-                pltpu.VMEM(flat, BF16),
-                pltpu.VMEM(flat, BF16),
                 pltpu.VMEM((batch, head, seq_local * kv_local), BF16),
                 pltpu.VMEM((PLANE * 16, head), F32),
                 pltpu.VMEM((32, head), F32),
@@ -376,20 +403,21 @@
             ]
         )
         any_space = pl.BlockSpec(memory_space=pl.ANY)
-        return pl.pallas_call(
-            update_kernel,
+        y, k_next, v_next = pl.pallas_call(
+            store_kernel,
             out_shape=[
                 jax.ShapeDtypeStruct(hidden.shape, BF16),
-                jax.ShapeDtypeStruct(k_cache.shape, BF16),
-                jax.ShapeDtypeStruct(v_cache.shape, BF16),
+                jax.ShapeDtypeStruct(flat, BF16),
+                jax.ShapeDtypeStruct(flat, BF16),
             ],
-            in_specs=[vmem] * 5 + [pl.BlockSpec(memory_space=pltpu.SMEM)],
+            in_specs=[vmem] * 3,
             out_specs=[any_space] * 3,
-            scratch_shapes=[dma, dma((2, batch, 3))],
+            scratch_shapes=[dma((2 * batch + 1,))],
             compiler_params=pltpu.CompilerParams(vmem_limit_bytes=16 << 20),
             cost_estimate=pl.CostEstimate(flops=1_000_000, bytes_accessed=8_000_000, transcendentals=0),
-            name="cache_update",
-        )(y, k_cache, v_cache, k_new, v_new, positions)
+            name="cache_store",
+        )(y, k_next, v_next)
+        return y, k_next.reshape(k_cache.shape), v_next.reshape(v_cache.shape)
 
     cache_spec = P("dp", "sp", "tp", None)
     specs_in = (P("dp", None), P(None), P(None, "tp"), P(None, "tp"), P(None, "tp"), P("tp", None), cache_spec, cache_spec, P("dp"))

time: 39.1 us -> 38.2 us (0.977)
  Pallas kernels: 38.3 us -> 37.5 us
    pallas_call x1, Pallas kernels: 2.88 us -> 2.09 us  [local_step(): pl.pallas_call(store_kernel, out_shape=[jax.ShapeDtypeStruct(hidden.shape...]
where the time goes in v3:
time: 38.2 us; the launch traced here: 38.1 us
  Pallas kernels  37.5 us (98%)
  between operations  0.64 us (2%)
    pallas_call x1, Pallas kernels, local_step(): pl.pallas_call(attention_kernel, out_shape=[jax.ShapeDtypeStruct(hidden.s...  35.4 us
    pallas_call x1, Pallas kernels, local_step(): pl.pallas_call(store_kernel, out_shape=[jax.ShapeDtypeStruct(hidden.shape...  2.09 us

profile of v3, /device:TPU:1, one launch (start us, length us, event | category | flops | bytes accessed | tf_op | source)
XLA Modules:
  0.0 38.1 jit_solution(18436675819215436224)
XLA Ops:
  0.6 35.4 %attention_step.1 = (bf16[4,8192]{1,0:T(4,128)(2,1)S(1)}, bf16[4,2048,128]{2,1,0:T(8,128)(2,1)S(1)}, bf16[4,2048,128]{2,1,0:T(8,128)(2,1)S(1)}) custom-call(bf16[4,8192]{1,0:T(4,128)(2,1)} %hidden_hbm.1, f32[1,8192]{1,0:T(1,128)} %bitcast.7, f32[1,128]{1,0:T(1,128)} %constant.2.clone.freq_hbm, s32[4]{0:T(128)} %pos_hbm.1, bf16[8192,4096]{1,0:T(8,128)(2,1)} %wq_hbm.1, ...), custom_call_target="tpu_custom_call" | custom-call | flops 20000000000 | bytes 20000000 | tf_op jit(solution)/shard_map/attention_step/pallas_call | solution.py:357
  36.0 2.1 %cache_store.1 = (bf16[4,8192]{1,0:T(4,128)(2,1)}, bf16[4,2048,128]{2,1,0:T(8,128)(2,1)}, bf16[4,2048,128]{2,1,0:T(8,128)(2,1)}) custom-call(bf16[4,8192]{1,0:T(4,128)(2,1)S(1)} %get-tuple-element.9.y_ref, bf16[4,2048,128]{2,1,0:T(8,128)(2,1)S(1)} %get-tuple-element.10.k_ref, bf16[4,2048,128]{2,1,0:T(8,128)(2,1)S(1)} %get-tuple-element.11.v_ref), custom_call_target="tpu_custom_call" | custom-call | flops 1000000 | bytes 8000000 | tf_op jit(solution)/shard_map/cache_store/pallas_call | solution.py:406

commit v4 on v3

--- a/solution.py
+++ b/solution.py
@@ -31,7 +31,7 @@
 def attention_kernel(
     hidden_hbm, gain_hbm, freq_hbm, pos_hbm, wq_hbm, wk_hbm, wv_hbm, wo_hbm, k_hbm, v_hbm,
     out_ref, kbuf, vbuf,
-    hid, gain, freq, wq, wk, wv, wo, kturn, gathered, fresh, rows, x0, x1, x2, x3, x4, x5, x6, x7, x8, orow,
+    hid, gain, freq, wq, wk, wv, wo, kturn, gathered, fresh, rows, x0, x1, x2, x3, x4, x5, x6, x7, x8, orow, stat, orow2,
     ypart, ypeer, yall, pos, sems, wq_sems, part_send, part_recv, qsend, qrecv, tpsend, tprecv, ysend, yrecv,
 ):
     batch, d_model = hid.shape
@@ -66,12 +66,11 @@
         cp.start()
     q_cols = pl.ds(pl.multiple_of(cell * 256, 256), 256)
     q_rows = d_model // CHUNKS
-    cp_wq = [
-        pltpu.make_async_copy(
-            wq_hbm.at[pl.ds(c * q_rows, q_rows), q_cols], wq.at[pl.ds(c * q_rows, q_rows), :], wq_sems.at[c]
-        )
-        for c in range(CHUNKS)
-    ]
+
+    def copy_wq(c):
+        here = pl.ds(pl.multiple_of(c * q_rows, q_rows), q_rows)
+        return pltpu.make_async_copy(wq_hbm.at[here, q_cols], wq.at[here, :], wq_sems.at[c])
+
     kv_depth = d_model // SIDE
     kv_rows = pl.ds(pl.multiple_of(lx * kv_depth, kv_depth), kv_depth)
     kv_cols = pl.ds(pl.multiple_of(ly * head, head), head)
@@ -79,8 +78,8 @@
     cp_wv = pltpu.make_async_copy(wv_hbm.at[kv_rows, kv_cols], wv, sems.at[5])
     cp_wk.start()
     cp_wv.start()
-    for cp in cp_wq:
-        cp.start()
+    for c in range(CHUNKS):
+        copy_wq(c).start()
     cp_k = pltpu.make_async_copy(k_hbm, kbuf, sems.at[6])
     cp_v = pltpu.make_async_copy(v_hbm, vbuf, sems.at[7])
     n_cols = wo.shape[1]
@@ -106,24 +105,28 @@
     cp_wv.wait()
     k_part = jnp.dot(normed_kv, wk[...], preferred_element_type=F32)
     v_part = jnp.dot(normed_kv, wv[...], preferred_element_type=F32)
-    q_acc = [jnp.zeros((batch, 256), F32), jnp.zeros((batch, 256), F32)]
-    for c in range(CHUNKS):
-        if c == 2:
-            cp_pos.wait()
-            cp_freq.wait()
-            row4 = lax.broadcasted_iota(jnp.int32, (batch, head), 0)
-            lane4 = lax.broadcasted_iota(jnp.int32, (batch, head), 1)
-            pos_rows = jnp.zeros((batch, head), jnp.int32)
-            for b in range(batch):
-                pos_rows = jnp.where(row4 == b, pos[b], pos_rows)
-            angles = pos_rows.astype(F32) * freq[...]
-            cosine = jnp.cos(angles)
-            sine = jnp.sin(angles)
-            sine = jnp.where(lane4 < head // 2, -sine, sine)
-        cp_wq[c].wait()
+    cp_pos.wait()
+    cp_freq.wait()
+    row4 = lax.broadcasted_iota(jnp.int32, (batch, head), 0)
+    lane4 = lax.broadcasted_iota(jnp.int32, (batch, head), 1)
+    pos_rows = jnp.zeros((batch, head), jnp.int32)
+    for b in range(batch):
+        pos_rows = jnp.where(row4 == b, pos[b], pos_rows)
+    angles = pos_rows.astype(F32) * freq[...]
+    cosine = jnp.cos(angles)
+    sine = jnp.sin(angles)
+    sine = jnp.where(lane4 < head // 2, -sine, sine)
+
+    def project(c, acc):
+        at = pl.multiple_of(c * q_rows, q_rows)
+        copy_wq(c).wait()
+        acc = list(acc)
         for u in range(2):
-            lo, hi = c * q_rows + u * q_rows // 2, c * q_rows + (u + 1) * q_rows // 2
-            q_acc[u] += jnp.dot(normed[:, lo:hi], wq[lo:hi, :], preferred_element_type=F32)
+            here = pl.ds(at + u * (q_rows // 2), q_rows // 2)
+            acc[u] += jnp.dot(rows[:, here].astype(BF16), wq[here, :], preferred_element_type=F32)
+        return tuple(acc)
+
+    q_acc = lax.fori_loop(0, CHUNKS, project, (jnp.zeros((batch, 256), F32), jnp.zeros((batch, 256), F32)))
     cp_k.start()
     cp_v.start()
 
@@ -174,8 +177,8 @@
     pad = jnp.zeros((12, head), F32)
     dims_last = (((1,), (1,)), ((), ()))
     cp_v.wait()
-    acc_rows, m_rows, l_rows = [], [], []
-    for b in range(batch):
+
+    def attend(b):
         k_b = jnp.concatenate([fresh[pl.ds(b, 4, stride=4), :], pad], axis=0).astype(BF16)
         v_b = jnp.concatenate([fresh[pl.ds(16 + b, 4, stride=4), :], pad], axis=0).astype(BF16)
         q_b = jnp.concatenate(
@@ -203,8 +206,7 @@
         total = p
         while len(total) > 1:
             total = [total[i] + total[i + 1] for i in range(0, len(total), 2)]
-        l_rows.append(jnp.sum(total[0], axis=-1, keepdims=True) + jnp.sum(p_new, axis=-1, keepdims=True))
-        m_rows.append(m)
+        l = jnp.sum(total[0], axis=-1, keepdims=True) + jnp.sum(p_new, axis=-1, keepdims=True)
         half_tiles = tiles // 2
         pv = [
             jnp.dot(
@@ -214,12 +216,18 @@
             )
             for u in range(2)
         ]
-        acc_rows.append(pv[0] + pv[1] + jnp.dot(p_new.astype(BF16), v_b, preferred_element_type=F32))
-    acc_t = jnp.concatenate(acc_rows, axis=0).T
-    m_col = jnp.concatenate(m_rows, axis=0)
-    l_col = jnp.concatenate(l_rows, axis=0)
-    stat_lane = lax.broadcasted_iota(jnp.int32, (128, 128), 1)
-    stat_t = jnp.where(stat_lane == 0, m_col, l_col).T[0:8]
+        here = pl.ds(pl.multiple_of(b * 32, 32), 32)
+        orow[here, :] = pv[0] + pv[1] + jnp.dot(p_new.astype(BF16), v_b, preferred_element_type=F32)
+        stat[here, :] = jnp.where(lane == 0, m, l)
+
+    def attend_some(g, carry):
+        for i in range(4):
+            attend(g * 4 + i)
+        return carry
+
+    lax.fori_loop(0, batch // 4, attend_some, 0)
+    acc_t = orow[...].T
+    stat_t = stat[...].T[0:8]
 
     parts = (x0, x1, x2, x3, x4, x5, x6, x7, x8)
 
@@ -239,22 +247,29 @@
             parts[p][0, slot, dims:dims + 8, :] = stat_t
         send_part(p, 0)
 
-    tile_pos = lax.broadcasted_iota(jnp.int32, (16, head), 0) >> 2
+    tile_pos = (lax.broadcasted_iota(jnp.int32, (16, head), 0) >> 2).astype(F32)
     block = 256
-    for buf, first in ((kbuf, 0), (vbuf, 16)):
+
+    def patch_cache(buf, first):
         for b in range(batch):
             new4 = fresh[pl.ds(first + b, 4, stride=4), :]
             new16 = jnp.concatenate([new4] * 4, axis=0).astype(BF16)
             spot = pos[b] - base
 
-            def patch(i, carry, buf=buf, b=b, new16=new16, spot=spot):
-                for j in range(block // 16):
-                    at = pl.ds(pl.multiple_of(i * block + j * 16, 16), 16)
-                    hit = tile_pos == spot - i * (block // 4) - 4 * j
-                    buf[b, at, :] = jnp.where(hit, new16, buf[b, at, :])
+            def patch(i, carry, b=b, new16=new16, spot=spot):
+                ahead = jnp.clip(spot - i * (block // 4), -1, block // 4).astype(F32)
+                ahead = (ahead - tile_pos).astype(BF16)
+                at = pl.ds(pl.multiple_of(i * block, block), block)
+                old = buf[b, at, :]
+                buf[b, at, :] = jnp.concatenate(
+                    [jnp.where(ahead == 4 * j, new16, old[16 * j:16 * (j + 1)]) for j in range(block // 16)], axis=0
+                )
                 return carry
 
             lax.fori_loop(0, cols // block, patch, 0)
+
+    patch_cache(vbuf, 16)
+    patch_cache(kbuf, 0)
 
     o_parts = []
     row8 = lax.broadcasted_iota(jnp.int32, (8, 128), 0)
@@ -288,23 +303,29 @@
     cp_wo.wait()
     o_rows = wo.shape[0] // CHUNKS
     half = n_cols // HALVES
-    cp_tp = []
-    for u in range(HALVES):
+
+    def copy_tp(u):
+        return pltpu.make_async_remote_copy(
+            src_ref=ypart.at[u], dst_ref=ypeer.at[u], send_sem=tpsend.at[u], recv_sem=tprecv.at[u],
+            device_id={"sp": me, "tp": 1 - core},
+        )
+
+    def project_out(u, carry):
+        here = pl.ds(pl.multiple_of(u * half, half), half)
         y = [jnp.zeros((batch, half), F32), jnp.zeros((batch, half), F32)]
         for c in range(CHUNKS):
             y[c % 2] += jnp.dot(
-                attn[:, c * o_rows:(c + 1) * o_rows],
-                wo[c * o_rows:(c + 1) * o_rows, u * half:(u + 1) * half],
+                orow2[:, c * o_rows:(c + 1) * o_rows],
+                wo[c * o_rows:(c + 1) * o_rows, here],
                 preferred_element_type=F32,
             )
         ypart[u] = y[0] + y[1]
-        cp_tp.append(
-            pltpu.make_async_remote_copy(
-                src_ref=ypart.at[u], dst_ref=ypeer.at[u], send_sem=tpsend.at[u], recv_sem=tprecv.at[u],
-                device_id={"sp": me, "tp": 1 - core},
-            )
-        )
-        cp_tp[u].start()
+        copy_tp(u).start()
+        return carry
+
+    orow2[...] = attn
+    lax.fori_loop(0, HALVES, project_out, 0)
+    cp_tp = [copy_tp(u) for u in range(HALVES)]
     for u in range(HALVES):
         cp_tp[u].wait_recv()
         yall[u, cell] = ypart[u] + ypeer[u]
@@ -377,6 +398,8 @@
                 pltpu.VMEM((batch, d_model), F32),
                 *[pltpu.VMEM((3, SIDE, d + 8 * stats, 128), F32) for _, d, stats in PARTS],
                 pltpu.VMEM((128, 128), F32),
+                pltpu.VMEM((128, 128), F32),
+                pltpu.VMEM((batch, w_out.shape[0]), BF16),
                 pltpu.VMEM((HALVES, batch, n_cols // HALVES), F32),
                 pltpu.VMEM((HALVES, batch, n_cols // HALVES), F32),
                 pltpu.VMEM((HALVES, PLANE, batch, n_cols // HALVES), F32),

time: 38.2 us -> 37.6 us (0.984)
  Pallas kernels: 37.5 us -> 36.8 us
    pallas_call x1, Pallas kernels: 35.4 us -> 34.7 us  [local_step(): pl.pallas_call(attention_kernel, out_shape=[jax.ShapeDtypeStruct(hidden.s...]
where the time goes in v4:
time: 37.6 us; the launch traced here: 37.4 us
  Pallas kernels  36.8 us (98%)
  between operations  0.64 us (2%)
    pallas_call x1, Pallas kernels, local_step(): pl.pallas_call(attention_kernel, out_shape=[jax.ShapeDtypeStruct(hidden.s...  34.7 us
    pallas_call x1, Pallas kernels, local_step(): pl.pallas_call(store_kernel, out_shape=[jax.ShapeDtypeStruct(hidden.shape...  2.09 us

profile of v4, /device:TPU:1, one launch (start us, length us, event | category | flops | bytes accessed | tf_op | source)
XLA Modules:
  0.0 37.4 jit_solution(10661857726276479944)
XLA Ops:
  0.6 34.7 %attention_step.1 = (bf16[4,8192]{1,0:T(4,128)(2,1)S(1)}, bf16[4,2048,128]{2,1,0:T(8,128)(2,1)S(1)}, bf16[4,2048,128]{2,1,0:T(8,128)(2,1)S(1)}) custom-call(bf16[4,8192]{1,0:T(4,128)(2,1)} %hidden_hbm.1, f32[1,8192]{1,0:T(1,128)} %bitcast.7, f32[1,128]{1,0:T(1,128)} %constant.2.clone.freq_hbm, s32[4]{0:T(128)} %pos_hbm.1, bf16[8192,4096]{1,0:T(8,128)(2,1)} %wq_hbm.1, ...), custom_call_target="tpu_custom_call" | custom-call | flops 20000000000 | bytes 20000000 | tf_op jit(solution)/shard_map/attention_step/pallas_call | solution.py:378
  35.4 2.1 %cache_store.1 = (bf16[4,8192]{1,0:T(4,128)(2,1)}, bf16[4,2048,128]{2,1,0:T(8,128)(2,1)}, bf16[4,2048,128]{2,1,0:T(8,128)(2,1)}) custom-call(bf16[4,8192]{1,0:T(4,128)(2,1)S(1)} %get-tuple-element.9.y_ref, bf16[4,2048,128]{2,1,0:T(8,128)(2,1)S(1)} %get-tuple-element.10.k_ref, bf16[4,2048,128]{2,1,0:T(8,128)(2,1)S(1)} %get-tuple-element.11.v_ref), custom_call_target="tpu_custom_call" | custom-call | flops 1000000 | bytes 8000000 | tf_op jit(solution)/shard_map/cache_store/pallas_call | solution.py:429

commit v5 on v4

--- a/solution.py
+++ b/solution.py
@@ -18,7 +18,7 @@
     (0, 16, False), (1, 8, False), (2, 8, False),
 )
 STARTS = tuple(sum(d for _, d, _ in PARTS[:i]) for i in range(len(PARTS)))
-HALVES = 2
+HALVES = 1
 CHUNKS = 8
 BF16 = jnp.bfloat16
 F32 = jnp.float32
@@ -31,7 +31,7 @@
 def attention_kernel(
     hidden_hbm, gain_hbm, freq_hbm, pos_hbm, wq_hbm, wk_hbm, wv_hbm, wo_hbm, k_hbm, v_hbm,
     out_ref, kbuf, vbuf,
-    hid, gain, freq, wq, wk, wv, wo, kturn, gathered, fresh, rows, x0, x1, x2, x3, x4, x5, x6, x7, x8, orow, stat, orow2,
+    hid, gain, freq, wq, wk, wv, wo, kturn, gathered, fresh, rows, x0, x1, x2, x3, x4, x5, x6, x7, x8, orow, stat,
     ypart, ypeer, yall, pos, sems, wq_sems, part_send, part_recv, qsend, qrecv, tpsend, tprecv, ysend, yrecv,
 ):
     batch, d_model = hid.shape
@@ -178,9 +178,10 @@
     dims_last = (((1,), (1,)), ((), ()))
     cp_v.wait()
 
-    def attend(b):
+    half_tiles = tiles // 2
+
+    def scores(b):
         k_b = jnp.concatenate([fresh[pl.ds(b, 4, stride=4), :], pad], axis=0).astype(BF16)
-        v_b = jnp.concatenate([fresh[pl.ds(16 + b, 4, stride=4), :], pad], axis=0).astype(BF16)
         q_b = jnp.concatenate(
             [gathered[pl.ds(b, 16, stride=16), :], gathered[pl.ds(4 + b, 16, stride=16), :]], axis=0
         ).astype(BF16)
@@ -194,8 +195,11 @@
         s_new = jnp.where(valid_new, s_new, NEG_BIG)
         s = []
         for i in range(tiles):
-            u, j = divmod(i, tiles // 2)
+            u, j = divmod(i, half_tiles)
             s.append(jnp.where(column < limit - 128 * i, s_halves[u][:, 128 * j:128 * (j + 1)], NEG_BIG))
+        return s, s_new
+
+    def weights(b, s, s_new):
         top = s
         while len(top) > 1:
             top = [jnp.maximum(top[i], top[i + 1]) for i in range(0, len(top), 2)]
@@ -207,25 +211,24 @@
         while len(total) > 1:
             total = [total[i] + total[i + 1] for i in range(0, len(total), 2)]
         l = jnp.sum(total[0], axis=-1, keepdims=True) + jnp.sum(p_new, axis=-1, keepdims=True)
-        half_tiles = tiles // 2
+        stat[32 * b:32 * (b + 1), :] = jnp.where(lane == 0, m, l)
+        halves = [
+            jnp.concatenate([pi.astype(BF16) for pi in p[u * half_tiles:(u + 1) * half_tiles]], axis=1) for u in range(2)
+        ]
+        return halves, p_new.astype(BF16)
+
+    def values(b, halves, p_new):
+        v_b = jnp.concatenate([fresh[pl.ds(16 + b, 4, stride=4), :], pad], axis=0).astype(BF16)
         pv = [
-            jnp.dot(
-                jnp.concatenate([pi.astype(BF16) for pi in p[u * half_tiles:(u + 1) * half_tiles]], axis=1),
-                vbuf[b, u * cols // 2:(u + 1) * cols // 2, :],
-                preferred_element_type=F32,
-            )
-            for u in range(2)
+            jnp.dot(halves[u], vbuf[b, u * cols // 2:(u + 1) * cols // 2, :], preferred_element_type=F32) for u in range(2)
         ]
-        here = pl.ds(pl.multiple_of(b * 32, 32), 32)
-        orow[here, :] = pv[0] + pv[1] + jnp.dot(p_new.astype(BF16), v_b, preferred_element_type=F32)
-        stat[here, :] = jnp.where(lane == 0, m, l)
-
-    def attend_some(g, carry):
-        for i in range(4):
-            attend(g * 4 + i)
-        return carry
-
-    lax.fori_loop(0, batch // 4, attend_some, 0)
+        orow[32 * b:32 * (b + 1), :] = pv[0] + pv[1] + jnp.dot(p_new, v_b, preferred_element_type=F32)
+
+    ready = scores(0)
+    for b in range(batch):
+        coming = scores(b + 1) if b + 1 < batch else None
+        values(b, *weights(b, *ready))
+        ready = coming
     acc_t = orow[...].T
     stat_t = stat[...].T[0:8]
 
@@ -310,21 +313,16 @@
             device_id={"sp": me, "tp": 1 - core},
         )
 
-    def project_out(u, carry):
-        here = pl.ds(pl.multiple_of(u * half, half), half)
-        y = [jnp.zeros((batch, half), F32), jnp.zeros((batch, half), F32)]
+    for u in range(HALVES):
+        y = jnp.zeros((batch, half), F32)
         for c in range(CHUNKS):
-            y[c % 2] += jnp.dot(
-                orow2[:, c * o_rows:(c + 1) * o_rows],
-                wo[c * o_rows:(c + 1) * o_rows, here],
+            y += jnp.dot(
+                attn[:, c * o_rows:(c + 1) * o_rows],
+                wo[c * o_rows:(c + 1) * o_rows, u * half:(u + 1) * half],
                 preferred_element_type=F32,
             )
-        ypart[u] = y[0] + y[1]
+        ypart[u] = y
         copy_tp(u).start()
-        return carry
-
-    orow2[...] = attn
-    lax.fori_loop(0, HALVES, project_out, 0)
     cp_tp = [copy_tp(u) for u in range(HALVES)]
     for u in range(HALVES):
         cp_tp[u].wait_recv()
@@ -399,7 +397,6 @@
                 *[pltpu.VMEM((3, SIDE, d + 8 * stats, 128), F32) for _, d, stats in PARTS],
                 pltpu.VMEM((128, 128), F32),
                 pltpu.VMEM((128, 128), F32),
-                pltpu.VMEM((batch, w_out.shape[0]), BF16),
                 pltpu.VMEM((HALVES, batch, n_cols // HALVES), F32),
                 pltpu.VMEM((HALVES, batch, n_cols // HALVES), F32),
                 pltpu.VMEM((HALVES, PLANE, batch, n_cols // HALVES), F32),

time: 37.6 us -> 36.6 us (0.973)
  Pallas kernels: 36.8 us -> 35.9 us
    pallas_call x1, Pallas kernels: 34.7 us -> 33.8 us  [local_step(): pl.pallas_call(attention_kernel, out_shape=[jax.ShapeDtypeStruct(hidden.s...]
where the time goes in v5:
time: 36.6 us; the launch traced here: 36.5 us
  Pallas kernels  35.9 us (98%)
  between operations  0.64 us (2%)
    pallas_call x1, Pallas kernels, local_step(): pl.pallas_call(attention_kernel, out_shape=[jax.ShapeDtypeStruct(hidden.s...  33.8 us
    pallas_call x1, Pallas kernels, local_step(): pl.pallas_call(store_kernel, out_shape=[jax.ShapeDtypeStruct(hidden.shape...  2.09 us

profile of v5, /device:TPU:1, one launch (start us, length us, event | category | flops | bytes accessed | tf_op | source)
XLA Modules:
  0.0 36.5 jit_solution(4591402430411313046)
XLA Ops:
  0.6 33.8 %attention_step.1 = (bf16[4,8192]{1,0:T(4,128)(2,1)S(1)}, bf16[4,2048,128]{2,1,0:T(8,128)(2,1)S(1)}, bf16[4,2048,128]{2,1,0:T(8,128)(2,1)S(1)}) custom-call(bf16[4,8192]{1,0:T(4,128)(2,1)} %hidden_hbm.1, f32[1,8192]{1,0:T(1,128)} %bitcast.7, f32[1,128]{1,0:T(1,128)} %constant.2.clone.freq_hbm, s32[4]{0:T(128)} %pos_hbm.1, bf16[8192,4096]{1,0:T(8,128)(2,1)} %wq_hbm.1, ...), custom_call_target="tpu_custom_call" | custom-call | flops 20000000000 | bytes 20000000 | tf_op jit(solution)/shard_map/attention_step/pallas_call | solution.py:376
  34.4 2.1 %cache_store.1 = (bf16[4,8192]{1,0:T(4,128)(2,1)}, bf16[4,2048,128]{2,1,0:T(8,128)(2,1)}, bf16[4,2048,128]{2,1,0:T(8,128)(2,1)}) custom-call(bf16[4,8192]{1,0:T(4,128)(2,1)S(1)} %get-tuple-element.9.y_ref, bf16[4,2048,128]{2,1,0:T(8,128)(2,1)S(1)} %get-tuple-element.10.k_ref, bf16[4,2048,128]{2,1,0:T(8,128)(2,1)S(1)} %get-tuple-element.11.v_ref), custom_call_target="tpu_custom_call" | custom-call | flops 1000000 | bytes 8000000 | tf_op jit(solution)/shard_map/cache_store/pallas_call | solution.py:426
